TPU v7x, 32 devices: a whole 2x2x4 slice. The times are simulated.
32 devices in a mesh: pp: 4 (over x, core), tp: 4 (over z), dp: 2 (over y).
Axes of the slice: x: 2, y: 2, z: 4, core: 2. Of those that a mesh axis runs over, the one named last changes fastest.
Arguments:
- act_in: bfloat16 [4, 2, 128, 4096], P('pp', 'dp', 'tp'), may hold values from -6 to 6
- stash_in: bfloat16 [4, 2, 128, 4096], P('pp', 'dp', 'tp'), may hold values from -6 to 6
- grad_in: bfloat16 [4, 2, 128, 4096], P('pp', 'dp', 'tp'), may hold values from -6 to 6
- doc_ids: int32 [4, 2, 2, 128], P('pp', 'dp'), may hold values from 0 to 15, never falling along the last dimension, each value on 1 to 64 neighbouring positions
- query_weight: bfloat16 [4, 4096, 4096], P('pp', None, 'tp'), as said below
- key_weight: bfloat16 [4, 4096, 1024], P('pp', None, 'tp'), as said below
- value_weight: bfloat16 [4, 4096, 1024], P('pp', None, 'tp'), as said below
- out_weight: bfloat16 [4, 4096, 4096], P('pp', None, 'tp'), may hold values from -0.09375 to 0.09375
Outputs:
- act_out: bfloat16 [4, 2, 128, 4096], P('pp', 'dp', 'tp')
- grad_out: bfloat16 [4, 2, 128, 4096], P('pp', 'dp', 'tp')
- grad_query: float32 [4, 4096, 4096], P('pp', 'dp', 'tp')
- grad_key: float32 [4, 4096, 1024], P('pp', 'dp', 'tp')
- grad_value: float32 [4, 4096, 1024], P('pp', 'dp', 'tp')
Inputs may be any that keep to these rules, and one draw needn't show every extreme that they name: `doc_ids`: along each row of 128 positions the document numbers never fall. `query_weight`: entries of mean zero. `key_weight`: for each of the 8 key heads, its 1 stored copies (consecutive blocks of 128 columns) are equal; entries of mean zero. `value_weight`: for each of the 8 value heads, its 1 stored copies (consecutive blocks of 128 columns) are equal.
All inputs are finite; a program needn't handle non-finite values.
Results may differ from a plain program's by a relative error of at most 0.033.
Values may be sent and summed in bfloat16 or wider, within the bound.
A program may use at most 128 MiB of HBM per device.

v0:
```python
import functools
import math

import jax
import jax.numpy as jnp
from jax import lax
from jax.experimental import pallas as pl
from jax.experimental.pallas import tpu as pltpu
from jax.sharding import PartitionSpec as P

HEAD = 128


epsilon = 1e-05


def from_behind(value, axis, steps):
    count = lax.axis_size(axis)
    pairs = [(source, (source + steps) % count) for source in range(count)]
    return lax.ppermute(value, axis, pairs)


MESH = pl.DeviceIdType.MESH
VMEM_LIMIT = 60 * 1024 * 1024


def remote(source, target, send_sem, recv_sem, axis, device):
    return pltpu.make_async_remote_copy(
        src_ref=source,
        dst_ref=target,
        send_sem=send_sem,
        recv_sem=recv_sem,
        device_id={axis: device},
        device_id_type=MESH,
    )


def greet(n, copies, me, mine):
    barrier = pltpu.get_barrier_semaphore()

    @pl.when(me > 0)
    def _():
        pl.semaphore_signal(barrier, inc=1, device_id={"tp": me - 1}, device_id_type=MESH)

    @pl.when(me < n - 1)
    def _():
        pl.semaphore_signal(barrier, inc=1, device_id={"tp": me + 1}, device_id_type=MESH)

    for offset in range(1, copies):
        other = lax.rem(mine + offset, copies)
        pl.semaphore_signal(barrier, inc=1, device_id={"dp": other}, device_id_type=MESH)

    ends = jnp.where(me > 0, 1, 0) + jnp.where(me < n - 1, 1, 0)
    pl.semaphore_wait(barrier, ends + copies - 1)


def gather_kernel(
    n, copies,
    act, stash, grad, wq, wk, wv, wo,
    qb, kb, vb, qf, kf, vf, dm, ncols,
    full, normed, vq, vk, vv, vo, wsem, ss, rs, dss, drs,
):
    me = lax.axis_index("tp")
    mine = lax.axis_index("dp")
    rows, width = act.shape
    piece = width // copies
    loads = []
    for i, (hbm, vmem) in enumerate(((wq, vq), (wk, vk), (wv, vv), (wo, vo))):
        load = pltpu.make_async_copy(hbm, vmem, wsem.at[i])
        load.start()
        loads.append(load)
    greet(n, copies, me, mine)
    own = (act, stash, grad)

    def block(a, index):
        return full.at[a, pl.ds(pl.multiple_of(index * rows, rows), rows), :]

    def hop(a, side, step):
        toward = 1 if side == 0 else -1
        carried = me - toward * (step - 1)
        source = own[a] if step == 1 else block(a, carried)
        return remote(
            source, block(a, carried),
            ss.at[a, side, step - 1], rs.at[a, side, step - 1], "tp", me + toward,
        )

    def sends(side, step):
        if side == 0:
            return (me < n - 1) & (me - (step - 1) >= 0)
        return (me > 0) & (me + (step - 1) < n)

    def gets(side, step):
        return (me - step >= 0) if side == 0 else (me + step < n)

    def start(a, step):
        for side in range(2):
            @pl.when(sends(side, step))
            def _():
                hop(a, side, step).start()

    def arrive(a, step):
        for side in range(2):
            @pl.when(gets(side, step))
            def _():
                toward = 1 if side == 0 else -1
                landed = block(a, me - toward * step)
                remote(
                    landed, landed,
                    ss.at[a, side, step - 1], rs.at[a, side, step - 1], "tp",
                    jnp.where(me == 0, 1, me - 1),
                ).wait_recv()

            if step < n - 1:
                @pl.when(sends(side, step + 1))
                def _():
                    hop(a, side, step + 1).start()

    def place(a):
        full[a, pl.ds(pl.multiple_of(me * rows, rows), rows), :] = own[a][...]

    def multiply(left, right, out):
        tile = 256

        @pl.loop(0, right.shape[1] // tile)
        def _(t):
            columns = pl.ds(pl.multiple_of(t * tile, tile), tile)
            out[:, columns] = jnp.dot(
                left[...], right[:, columns], preferred_element_type=jnp.float32
            ).astype(jnp.bfloat16)

    def normalise(a):
        band = 16

        @pl.loop(0, full.shape[1] // band)
        def _(t):
            where = pl.ds(pl.multiple_of(t * band, band), band)
            wide = full[a, where, :].astype(jnp.float32)
            inverse = lax.rsqrt(jnp.mean(wide * wide, axis=-1, keepdims=True) + epsilon)
            normed[where, :] = (wide * inverse).astype(jnp.bfloat16)

    start(0, 1)
    start(1, 1)
    for a in range(3):
        place(a)
    for step in range(1, n):
        arrive(0, step)
    start(2, 1)
    arrive(1, 1)
    normalise(0)
    for load in loads:
        load.wait()
    multiply(normed, vq, qb)
    multiply(normed, vk, kb)
    multiply(normed, vv, vb)
    trades = []
    for offset in range(1, copies):
        other = lax.rem(mine + offset, copies)
        trade = remote(
            normed.at[:, pl.ds(pl.multiple_of(other * piece, piece), piece)],
            ncols.at[mine], dss.at[offset], drs.at[offset], "dp", other,
        )
        trade.start()
        trades.append(trade)
    ncols[mine] = normed[:, pl.ds(pl.multiple_of(mine * piece, piece), piece)]
    for step in range(2, n):
        arrive(1, step)
    arrive(2, 1)
    multiply(full.at[1], vo, dm)
    for step in range(2, n):
        arrive(2, step)
    for trade in trades:
        trade.wait()
    normalise(2)
    multiply(normed, vq, qf)
    multiply(normed, vk, kf)
    multiply(normed, vv, vf)
    for a in range(3):
        for step in range(1, n):
            for side in range(2):
                @pl.when(sends(side, step))
                def _():
                    hop(a, side, step).wait_send()


def gather_call(n, copies, act, grad, stash, wq, wk, wv, wo):
    rows, width = act.shape
    seq = rows * n
    bf = jnp.bfloat16
    vmem = pl.BlockSpec(memory_space=pltpu.VMEM)
    anywhere = pl.BlockSpec(memory_space=pl.ANY)
    shapes = [(seq, w.shape[1]) for w in (wq, wk, wv)] * 2 + [(seq, wo.shape[1])]
    shapes += [(copies, seq, width // copies)]
    sem = pltpu.SemaphoreType.DMA
    return pl.pallas_call(
        functools.partial(gather_kernel, n, copies),
        out_shape=[jax.ShapeDtypeStruct(shape, bf) for shape in shapes],
        in_specs=[vmem] * 3 + [anywhere] * 4,
        out_specs=[vmem] * len(shapes),
        scratch_shapes=[pltpu.VMEM((3, seq, width), bf), pltpu.VMEM((seq, width), bf)]
        + [pltpu.VMEM(w.shape, bf) for w in (wq, wk, wv, wo)]
        + [sem((4,)), sem((3, 2, n)), sem((3, 2, n)), sem((copies,)), sem((copies,))],
        compiler_params=pltpu.CompilerParams(
            collective_id=0, has_side_effects=True, vmem_limit_bytes=VMEM_LIMIT
        ),
        cost_estimate=pl.CostEstimate(
            flops=40_000_000_000, bytes_accessed=30_000_000, transcendentals=0
        ),
    )(stash, grad, act, wq, wk, wv, wo)


def scatter_kernel(
    n, copies,
    fsum, bsum, dq, dk, dv,
    fshare, bshare, aq, ak, av,
    slots, ss, rs, dss, drs,
):
    me = lax.axis_index("tp")
    mine = lax.axis_index("dp")
    rows, width = fshare.shape
    sums = (bsum, fsum)
    greet(n, copies, me, mine)
    trades = []
    for offset in range(1, copies):
        other = lax.rem(mine + offset, copies)
        for i, (source, target) in enumerate(((dq, aq), (dk, ak), (dv, av))):
            trade = remote(
                source, target.at[mine], dss.at[offset, i], drs.at[offset, i], "dp", other
            )
            trade.start()
            trades.append(trade)

    def copy(a, side, dest, first):
        toward = 1 if side == 0 else -1
        part = sums[a].at[pl.ds(dest * rows, rows), :]
        return remote(
            part if first else slots.at[a, side, dest], slots.at[a, side, dest],
            ss.at[a, side, dest], rs.at[a, side, dest], "tp", me + toward,
        )

    def landed(a, side, dest):
        slot = slots.at[a, side, dest]
        remote(
            slot, slot, ss.at[a, side, dest], rs.at[a, side, dest], "tp",
            jnp.where(me == 0, 1, me - 1),
        ).wait_recv()

    def roles(side, dest):
        if side == 0:
            return me == 0, (me > 0) & (me < dest)
        return me == n - 1, (me < n - 1) & (me > dest)

    routes = []
    for k in range(n - 1):
        for side in range(2):
            routes.append((side, n - 1 - k if side == 0 else k))
    for a in range(2):
        for side, dest in routes:
            first, middle = roles(side, dest)

            @pl.when(first)
            def _():
                copy(a, side, dest, True).start()

    aq[mine] = dq[...]
    ak[mine] = dk[...]
    av[mine] = dv[...]
    for a in range(2):
        for side, dest in routes:
            first, middle = roles(side, dest)

            @pl.when(middle)
            def _():
                landed(a, side, dest)
                slots[a, side, dest] = (
                    slots[a, side, dest].astype(jnp.float32)
                    + sums[a][dest * rows : (dest + 1) * rows, :].astype(jnp.float32)
                ).astype(jnp.bfloat16)
                copy(a, side, dest, False).start()

    for a, out in enumerate((bshare, fshare)):
        out[...] = sums[a][pl.ds(pl.multiple_of(me * rows, rows), rows), :].astype(jnp.float32)
        for side, dest in routes:
            @pl.when(me == dest)
            def _():
                landed(a, side, dest)
                out[...] += slots[a, side, dest].astype(jnp.float32)

    for a in range(2):
        for side, dest in routes:
            first, middle = roles(side, dest)

            @pl.when(first | middle)
            def _():
                copy(a, side, dest, False).wait_send()

    for trade in trades:
        trade.wait()


def scatter_call(n, copies, fsum, bsum, dq, dk, dv):
    seq, width = fsum.shape
    rows = seq // n
    vmem = pl.BlockSpec(memory_space=pltpu.VMEM)
    sem = pltpu.SemaphoreType.DMA
    return pl.pallas_call(
        functools.partial(scatter_kernel, n, copies),
        out_shape=[jax.ShapeDtypeStruct((rows, width), jnp.float32)] * 2
        + [jax.ShapeDtypeStruct((copies,) + g.shape, jnp.bfloat16) for g in (dq, dk, dv)],
        in_specs=[vmem] * 5,
        out_specs=[vmem] * 5,
        scratch_shapes=[
            pltpu.VMEM((2, 2, n, rows, width), jnp.bfloat16),
            sem((2, 2, n)), sem((2, 2, n)), sem((copies, 3)), sem((copies, 3)),
        ],
        compiler_params=pltpu.CompilerParams(
            collective_id=1, has_side_effects=True, vmem_limit_bytes=40 * 1024 * 1024
        ),
        cost_estimate=pl.CostEstimate(
            flops=30_000_000_000, bytes_accessed=10_000_000, transcendentals=0
        ),
    )(fsum, bsum, dq, dk, dv)


def weights_kernel(copies, ncols, aq, ak, av, gq, gk, gv):
    for right, out in ((aq, gq), (ak, gk), (av, gv)):
        total = None
        for i in range(copies):
            term = lax.dot_general(
                ncols[i], right[i], (((0,), (0,)), ((), ())),
                preferred_element_type=jnp.float32,
            ).astype(jnp.bfloat16).astype(jnp.float32)
            total = term if total is None else total + term
        out[...] = total


def weights_call(ncols, aq, ak, av):
    copies, seq, piece = ncols.shape
    tile = min(256, piece)
    whole = [
        pl.BlockSpec(g.shape, lambda t: (0, 0, 0)) for g in (aq, ak, av)
    ]
    outs = [jax.ShapeDtypeStruct((piece, g.shape[2]), jnp.float32) for g in (aq, ak, av)]
    return pl.pallas_call(
        functools.partial(weights_kernel, copies),
        grid=(piece // tile,),
        out_shape=outs,
        in_specs=[pl.BlockSpec((copies, seq, tile), lambda t: (0, 0, t))] + whole,
        out_specs=[pl.BlockSpec((tile, o.shape[1]), lambda t: (t, 0)) for o in outs],
        compiler_params=pltpu.CompilerParams(vmem_limit_bytes=40 * 1024 * 1024),
        cost_estimate=pl.CostEstimate(
            flops=2 * copies * seq * piece * sum(o.shape[1] for o in outs),
            bytes_accessed=4 * piece * sum(o.shape[1] for o in outs),
            transcendentals=0,
        ),
    )(ncols, aq, ak, av)


def norm_rows(token_rows):
    widened = token_rows.astype(jnp.float32)
    inverse = lax.rsqrt(jnp.mean(widened * widened, axis=-1, keepdims=True) + epsilon)
    return ((widened * inverse).astype(jnp.bfloat16), inverse)


def allowed(documents):
    length = documents.shape[0]
    position = jnp.arange(length, dtype=jnp.int32)
    return (position[None, :] <= position[:, None]) & (documents[:, None] == documents[None, :])


def contract_last(left_side, right_side):
    return lax.dot_general(
        left_side, right_side, (((1,), (1,)), ((), ())), preferred_element_type=jnp.float32
    )


def split_heads(queries, keys, values, kv_local):
    length = queries.shape[0]
    group_size = queries.shape[1] // (kv_local * HEAD)
    return (
        queries.reshape(length, kv_local, group_size, HEAD),
        keys.reshape(length, kv_local, HEAD),
        values.reshape(length, kv_local, HEAD),
    )


def attend_probs(query_heads, key_heads, allowed_pairs):
    scores = jnp.einsum(
        "ihgd,jhd->hgij", query_heads, key_heads, preferred_element_type=jnp.float32
    ) * (1.0 / math.sqrt(HEAD))
    scores = jnp.where(allowed_pairs, scores, -jnp.inf)
    row_max = jnp.max(scores, axis=-1, keepdims=True)
    weights = jnp.exp(scores - row_max)
    return (weights / jnp.sum(weights, axis=-1, keepdims=True)).astype(jnp.bfloat16)


def attend_back(dmixed, queries, keys, values, probs, kv_local):
    length = queries.shape[0]
    query_heads, key_heads, value_heads = split_heads(queries, keys, values, kv_local)
    dmixed_heads = dmixed.reshape(query_heads.shape)
    dprobs = jnp.einsum(
        "ihgd,jhd->hgij", dmixed_heads, value_heads, preferred_element_type=jnp.float32
    )
    weights = probs.astype(jnp.float32)
    inner = jnp.sum(weights * dprobs, axis=-1, keepdims=True)
    dscores = (weights * (dprobs - inner) * (1.0 / math.sqrt(HEAD))).astype(jnp.bfloat16)
    dqueries = jnp.einsum("hgij,jhd->ihgd", dscores, key_heads, preferred_element_type=jnp.float32)
    dkeys = jnp.einsum("hgij,ihgd->jhd", dscores, query_heads, preferred_element_type=jnp.float32)
    dvalues = jnp.einsum("hgij,ihgd->jhd", probs, dmixed_heads, preferred_element_type=jnp.float32)
    return (
        dqueries.astype(jnp.bfloat16).reshape(length, queries.shape[1]),
        dkeys.reshape(length, kv_local * HEAD),
        dvalues.reshape(length, kv_local * HEAD),
    )


def handoff(payload, offset):
    return from_behind(payload, "pp", offset)


def body(act_in, stash_in, grad_in, doc_ids, query_weight, key_weight, value_weight, out_weight):
    kv_local = key_weight.shape[2] // HEAD
    forward_rows = act_in[0, 0]
    backward_rows = stash_in[0, 0]
    grad_rows = grad_in[0, 0]
    w_query = query_weight[0]
    w_key = key_weight[0]
    w_value = value_weight[0]
    w_out = out_weight[0]
    n, copies = lax.axis_size("tp"), lax.axis_size("dp")
    (
        queries_back, keys_back, values_back, queries_ahead, keys_ahead, values_ahead,
        dmixed, normed_cols,
    ) = gather_call(
        n, copies, forward_rows, grad_rows, backward_rows, w_query, w_key, w_value, w_out
    )
    unused_normed, inverse_back = norm_rows(backward_rows)
    query_heads, key_heads, value_heads = split_heads(
        queries_ahead, keys_ahead, values_ahead, kv_local
    )
    probs_ahead = attend_probs(query_heads, key_heads, allowed(doc_ids[0, 0, 0]))
    mixed_ahead = jnp.einsum(
        "hgij,jhd->ihgd", probs_ahead, value_heads, preferred_element_type=jnp.float32
    )
    mixed_ahead = mixed_ahead.astype(jnp.bfloat16).reshape(queries_ahead.shape)
    forward_sum = contract_last(mixed_ahead, w_out)
    query_back_heads, key_back_heads, unused_values = split_heads(
        queries_back, keys_back, values_back, kv_local
    )
    probs_back = attend_probs(query_back_heads, key_back_heads, allowed(doc_ids[0, 0, 1]))
    dqueries, dkeys, dvalues = attend_back(
        dmixed, queries_back, keys_back, values_back, probs_back, kv_local
    )
    dkey_cols = dkeys.astype(jnp.bfloat16)
    dvalue_cols = dvalues.astype(jnp.bfloat16)
    dnormed = (
        contract_last(dqueries, w_query)
        + contract_last(dkey_cols, w_key)
        + contract_last(dvalue_cols, w_value)
    )
    forward_share, backward_share, all_queries, all_keys, all_values = scatter_call(
        n, copies, forward_sum.astype(jnp.bfloat16), dnormed.astype(jnp.bfloat16),
        dqueries, dkey_cols, dvalue_cols,
    )
    outgoing = (forward_rows.astype(jnp.float32) + forward_share).astype(jnp.bfloat16)
    scaled = backward_rows.astype(jnp.float32) * inverse_back
    grad_back = (
        grad_rows.astype(jnp.float32)
        + inverse_back
        * (backward_share - scaled * jnp.mean(backward_share * scaled, axis=-1, keepdims=True))
    ).astype(jnp.bfloat16)
    act_out = handoff(outgoing, 1)[None, None]
    grad_out = handoff(grad_back, -1)[None, None]
    grad_query, grad_key, grad_value = (
        grad[None] for grad in weights_call(normed_cols, all_queries, all_keys, all_values)
    )
    return (act_out, grad_out, grad_query, grad_key, grad_value)


def solution(mesh):
    placed = (
        P("pp", "dp", "tp", None),
        P("pp", "dp", "tp", None),
        P("pp", "dp", "tp", None),
        P("pp", "dp", None, None),
        P("pp", None, "tp"),
        P("pp", None, "tp"),
        P("pp", None, "tp"),
        P("pp", None, "tp"),
    )
    return jax.shard_map(
        body,
        mesh=mesh,
        in_specs=placed,
        out_specs=(
            P("pp", "dp", "tp", None),
            P("pp", "dp", "tp", None),
            P("pp", "dp", "tp"),
            P("pp", "dp", "tp"),
            P("pp", "dp", "tp"),
        ),
        check_vma=False,
    )
```

profile of v0, /device:TPU:1, one launch (start us, length us, event | category | flops | bytes accessed | tf_op | source)
XLA Modules:
  0.0 143.5 jit_solution(1329474443908314995)
XLA Ops:
  0.6 1.1 fusion.33
  1.7 0.8 slice_bitcast_fusion
  2.5 61.7 %shard_map.119 = (bf16[128,1024]{1,0:T(8,128)(2,1)}, bf16[128,256]{1,0:T(8,128)(2,1)}, bf16[128,256]{1,0:T(8,128)(2,1)}, bf16[128,1024]{1,0:T(8,128)(2,1)}, bf16...) custom-call(bf16[32,4096]{1,0:T(8,128)(2,1)} %bitcast.99, ...), custom_call_target="tpu_custom_call" | custom-call | flops 40000000000 | bytes 30000000 | tf_op jit(solution)/shard_map/pallas_call | solution.py:194
  64.2 0.9 reshape.67
  65.1 1.1 reshape.68
  66.4 0.3 fusion.60
  66.7 0.2 fusion.14
  67.7 0.4 fusion.65
  68.2 0.3 fusion.16
  68.5 0.3 convolution_convert_fusion.1
  68.8 0.2 fusion.17
  69.2 6.3 %fusion.54 = f32[128,4096]{1,0:T(8,128)S(1)} fusion(bf16[128,1024]{0,1:T(8,128)(2,1)S(1)} %bitcast.103, bf16[1,4096,1024]{2,1,0:T(8,128)(2,1)} %param.12), kind=kOutput, calls=%fused_computation.67 | convolution fusion | flops 1073741824 | bytes 10747904 | tf_op jit(solution)/shard_map/dot_general | solution.py:371
  75.9 0.3 convolution_convert_fusion.2
  76.3 6.4 %convolution_convert_fusion.fsum = bf16[128,4096]{1,0:T(8,128)(2,1)S(1)} fusion(bf16[128,1024]{0,1:T(8,128)(2,1)S(1)} %bitcast.108, bf16[1,4096,1024]{2,1,0:T(8,128)(2,1)} %param.15), kind=kOutput, calls=%fused_computation.6 | convolution fusion | flops 1074266112 | bytes 9699328 | tf_op jit(solution)/shard_map/dot_general | solution.py:371
  82.7 0.8 convolution_add_fusion.1
  83.5 0.8 copy-done.3
  84.3 0.8 fusion.3.bsum
  85.1 40.6 %shard_map.120 = (f32[32,4096]{1,0:T(8,128)S(1)}, f32[32,4096]{1,0:T(8,128)S(1)}, bf16[2,128,1024]{2,1,0:T(8,128)(2,1)S(1)}, bf16[2,128,256]{2,1,0:T(8,128)(2,1)S(1)}, bf16[2,128,256]{2,1,0:T(8,128)(2,1)S(1)}) custom-call(bf16[128,4096]{1,0:T(8,128)(2,1)S(1)} %convolution_convert_fusion.fsum, bf16[128,4096]{1,0:T(8,128)(2,1)S(1)} %fusion.3.bsum, ...), custom_call_target="tpu_custom_call" | custom-call | flops 30000001024 | bytes 10000000 | tf_op jit(solution)/shard_map/pallas_call | solution.py:305
  125.8 0.3 fusion.28
  126.2 6.9 %collective-permute-start.1 = (bf16[32,4096]{1,0:T(8,128)(2,1)S(1)}, bf16[32,4096]{1,0:T(8,128)(2,1)S(1)}, u32[]{:S(2)}, u32[]{:S(2)}) collective-permute-start(bf16[32,4096]{1,0:T(8,128)(2,1)S(1)} %fusion.32), channel_id=1, source_target_pairs={{0,24},{8,0},{16,8},{24,16},{1,25},{9,1},{17,9},{25,17},{2,26},{10... | collective-permute-start | bytes 786440 | tf_op jit(solution)/shard_map/ppermute | solution.py:20
  133.2 1.5 %collective-permute-start = (bf16[32,4096]{1,0:T(8,128)(2,1)S(1)}, bf16[32,4096]{1,0:T(8,128)(2,1)S(1)}, u32[]{:S(2)}, u32[]{:S(2)}) collective-permute-start(bf16[32,4096]{1,0:T(8,128)(2,1)S(1)} %add_convert_fusion), channel_id=1, source_target_pairs={{0,8},{8,16},{16,24},{24,0},{1,9},{9,17},{17,25},{25,1},{2,10},{10... | collective-permute-start | bytes 786440 | tf_op jit(solution)/shard_map/ppermute | solution.py:20
  134.8 7.3 %shard_map.121 = (f32[2048,1024]{1,0:T(8,128)}, f32[2048,256]{1,0:T(8,128)}, f32[2048,256]{1,0:T(8,128)}) custom-call(bf16[2,128,2048]{2,1,0:T(8,128)(2,1)S(1)} %copy-done, bf16[2,128,1024]{2,1,0:T(8,128)(2,1)S(1)} %get-tuple-element.31.aq, bf16[2,128,256]{2,1,0:T(8,128)(2,1)S(1)} %get-tuple-element.32.ak, bf16[2,128,256]{2,1,0:T(8,128)(2,1)S(1)} %get-tuple-element.33.av), custom_call_target="tpu_custom_call" | custom-call | flops 1610612736 | bytes 12582912 | tf_op jit(solution)/shard_map/pallas_call | solution.py:343
  142.1 0.7 copy.71
  142.8 0.7 copy.72
  (39 shorter events, 1.7 us)
Async XLA Ops:
  64.2 2.8 %copy-start.10 = (bf16[128,256]{1,0:T(8,128)(2,1)S(1)}, bf16[128,256]{1,0:T(8,128)(2,1)}, u32[]{:S(2)}) copy-start(bf16[128,256]{1,0:T(8,128)(2,1)} %get-tuple-element.24) | copy-start | bytes 196612
  64.2 2.9 %copy-start.9 = (bf16[128,256]{1,0:T(8,128)(2,1)S(1)}, bf16[128,256]{1,0:T(8,128)(2,1)}, u32[]{:S(2)}) copy-start(bf16[128,256]{1,0:T(8,128)(2,1)} %get-tuple-element.26) | copy-start | bytes 196612
  64.2 3.0 %copy-start.5 = (bf16[128,1024]{1,0:T(8,128)(2,1)S(1)}, bf16[128,1024]{1,0:T(8,128)(2,1)}, u32[]{:S(2)}) copy-start(bf16[128,1024]{1,0:T(8,128)(2,1)} %get-tuple-element.25) | copy-start | bytes 786436
  64.2 3.1 %copy-start.4 = (bf16[128,1024]{1,0:T(8,128)(2,1)S(1)}, bf16[128,1024]{1,0:T(8,128)(2,1)}, u32[]{:S(2)}) copy-start(bf16[128,1024]{1,0:T(8,128)(2,1)} %get-tuple-element.27) | copy-start | bytes 786436
  69.2 6.4 %copy-start.8 = (bf16[128,256]{1,0:T(8,128)(2,1)S(1)}, bf16[128,256]{1,0:T(8,128)(2,1)}, u32[]{:S(2)}) copy-start(bf16[128,256]{1,0:T(8,128)(2,1)} %get-tuple-element.21) | copy-start | bytes 196612
  76.2 6.5 %copy-start.2 = (bf16[1,4096,256]{2,1,0:T(8,128)(2,1)S(1)}, bf16[1,4096,256]{2,1,0:T(8,128)(2,1)}, u32[]{:S(2)}) copy-start(bf16[1,4096,256]{2,1,0:T(8,128)(2,1)} %param.13) | copy-start | bytes 6291460
  82.7 1.6 %copy-start.3 = (bf16[1,4096,256]{2,1,0:T(8,128)(2,1)S(1)}, bf16[1,4096,256]{2,1,0:T(8,128)(2,1)}, u32[]{:S(2)}) copy-start(bf16[1,4096,256]{2,1,0:T(8,128)(2,1)} %param.14) | copy-start | bytes 6291460
  85.1 40.6 %copy-start.1 = (bf16[1,1,32,4096]{3,2,1,0:T(8,128)(2,1)S(1)}, bf16[1,1,32,4096]{3,2,1,0:T(8,128)(2,1)}, u32[]{:S(2)}) copy-start(bf16[1,1,32,4096]{3,2,1,0:T(8,128)(2,1)} %param.9) | copy-start | bytes 786436
  85.1 40.9 %copy-start.6 = (bf16[1,1,32,4096]{3,2,1,0:T(8,128)(2,1)S(1)}, bf16[1,1,32,4096]{3,2,1,0:T(8,128)(2,1)}, u32[]{:S(2)}) copy-start(bf16[1,1,32,4096]{3,2,1,0:T(8,128)(2,1)} %param.10) | copy-start | bytes 786436
  125.7 7.4 %copy-start.7 = (bf16[1,1,32,4096]{3,2,1,0:T(8,128)(2,1)S(1)}, bf16[1,1,32,4096]{3,2,1,0:T(8,128)(2,1)}, u32[]{:S(2)}) copy-start(bf16[1,1,32,4096]{3,2,1,0:T(8,128)(2,1)} %param.8) | copy-start | bytes 786436
  125.8 9.0 %copy-start = (bf16[2,128,2048]{2,1,0:T(8,128)(2,1)S(1)}, bf16[2,128,2048]{2,1,0:T(8,128)(2,1)}, u32[]{:S(2)}) copy-start(bf16[2,128,2048]{2,1,0:T(8,128)(2,1)} %get-tuple-element.30.ncols) | copy-start | bytes 3145732
  126.2 15.8 %collective-permute-start.1 = (bf16[32,4096]{1,0:T(8,128)(2,1)S(1)}, bf16[32,4096]{1,0:T(8,128)(2,1)S(1)}, u32[]{:S(2)}, u32[]{:S(2)}) collective-permute-start(bf16[32,4096]{1,0:T(8,128)(2,1)S(1)} %fusion.32), channel_id=1, source_target_pairs={{0,24},{8,0},{16,8},{24,16},{1,25},{9,1},{17,9},{25,17},{2,26},{10... | collective-permute-start | bytes 786440 | tf_op jit(solution)/shard_map/ppermute | solution.py:20
  133.2 8.8 %collective-permute-start = (bf16[32,4096]{1,0:T(8,128)(2,1)S(1)}, bf16[32,4096]{1,0:T(8,128)(2,1)S(1)}, u32[]{:S(2)}, u32[]{:S(2)}) collective-permute-start(bf16[32,4096]{1,0:T(8,128)(2,1)S(1)} %add_convert_fusion), channel_id=1, source_target_pairs={{0,8},{8,16},{16,24},{24,0},{1,9},{9,17},{17,25},{25,1},{2,10},{10... | collective-permute-start | bytes 786440 | tf_op jit(solution)/shard_map/ppermute | solution.py:20
where the time goes:
time: 144 us; the launch traced here: 143 us
  Pallas kernels  110 us (76%)
  matrix products  16.7 us (12%)
  starting transfers between devices  8.48 us (6%)
  local copies, waits for them, and re-layouts  5.99 us (4%)
  other arithmetic  1.78 us (1%)
    pallas_call x1, Pallas kernels, gather_call(): pl.pallas_call(functools.partial(gather_kernel, n, copies), out_shape=[ja...  61.7 us
    pallas_call x1, Pallas kernels, scatter_call(): pl.pallas_call(functools.partial(scatter_kernel, n, copies), out_shape=[j...  40.6 us
    dot_general x4, matrix products, contract_last(): lax.dot_general(left_side, right_side, (((1,), (1,)), ((), ())), preferre...  14.4 us
    ppermute x2, starting transfers between devices, from_behind(): return lax.ppermute(value, axis, pairs)  8.48 us
    pallas_call x1, Pallas kernels, weights_call(): pl.pallas_call(functools.partial(weights_kernel, copies), grid=(piece //...  7.29 us
  transfers between devices with their start and end apart: 2, of which 0 were waited for; matrix products, arithmetic and copies ran while one was open for 0% of the time, Pallas kernels for 5%

commit v1 on v0

v1 whole, which is shorter than its diff:
```python
import functools
import math

import jax
import jax.numpy as jnp
from jax import lax
from jax.experimental import pallas as pl
from jax.experimental.pallas import tpu as pltpu
from jax.sharding import PartitionSpec as P

HEAD = 128
epsilon = 1e-05
MESH = pl.DeviceIdType.MESH
VMEM_LIMIT = 62 * 1024 * 1024
bf16 = jnp.bfloat16
f32 = jnp.float32


def remote(source, target, send_sem, recv_sem, axis, device):
    return pltpu.make_async_remote_copy(
        src_ref=source,
        dst_ref=target,
        send_sem=send_sem,
        recv_sem=recv_sem,
        device_id={axis: device},
        device_id_type=MESH,
    )


def contract_last(left, right):
    return lax.dot_general(left, right, (((1,), (1,)), ((), ())), preferred_element_type=f32)


def contract_first(left, right):
    return lax.dot_general(left, right, (((0,), (0,)), ((), ())), preferred_element_type=f32)


def chunking(rows, width):
    return (2, 4) if rows * width >= 32 * 4096 else (1, 1)


def section_kernel(
    n, copies, stages, gather_parts, sum_parts,
    stash, grad, act, docs, wq, wk, wv, wo,
    act_out, grad_out, ncols, aq, ak, av,
    full, inv, vq, vk, vv, vo, q, k, v, dm, mixed, probs, dq, dk, dv,
    sums, slots, total, outgoing,
    wsem, ss, rs, ts, tr, dss, drs, hs, hr,
):
    me = lax.axis_index("tp")
    mine = lax.axis_index("dp")
    stage = lax.axis_index("pp")
    rows, width = act.shape
    seq = rows * n
    piece = width // copies
    kv_local = vk.shape[1] // HEAD
    group = vq.shape[1] // (kv_local * HEAD)
    scale = 1.0 / math.sqrt(HEAD)
    own = (stash, grad, act)

    loads = []
    for i, (hbm, vmem) in enumerate(((wq, vq), (wk, vk), (wv, vv), (wo, vo))):
        load = pltpu.make_async_copy(hbm, vmem, wsem.at[i])
        load.start()
        loads.append(load)

    barrier = pltpu.get_barrier_semaphore()

    @pl.when(me > 0)
    def _():
        pl.semaphore_signal(barrier, inc=1, device_id={"tp": me - 1}, device_id_type=MESH)

    @pl.when(me < n - 1)
    def _():
        pl.semaphore_signal(barrier, inc=1, device_id={"tp": me + 1}, device_id_type=MESH)

    for offset in range(1, copies):
        other = lax.rem(mine + offset, copies)
        pl.semaphore_signal(barrier, inc=1, device_id={"dp": other}, device_id_type=MESH)
    ahead, behind = lax.rem(stage + 1, stages), lax.rem(stage + stages - 1, stages)
    for other in (ahead, behind):
        pl.semaphore_signal(barrier, inc=1, device_id={"pp": other}, device_id_type=MESH)
    ends = jnp.where(me > 0, 1, 0) + jnp.where(me < n - 1, 1, 0)
    pl.semaphore_wait(barrier, ends + copies - 1 + 2)

    def at_rows(index):
        return pl.ds(pl.multiple_of(index * rows, rows), rows)

    def part(c, parts):
        return pl.ds(c * (width // parts), width // parts)

    def hop(a, side, step, c):
        toward = 1 if side == 0 else -1
        carried = me - toward * (step - 1)
        columns = part(c, gather_parts)
        target = full.at[a, at_rows(carried), columns]
        source = own[a].at[:, columns] if step == 1 else target
        return remote(
            source, target, ss.at[a, side, step - 1, c], rs.at[a, side, step - 1, c],
            "tp", me + toward,
        )

    def sends(side, step):
        if side == 0:
            return (me < n - 1) & (me - (step - 1) >= 0)
        return (me > 0) & (me + (step - 1) < n)

    def gets(side, step):
        return (me - step >= 0) if side == 0 else (me + step < n)

    def start(a):
        for c in range(gather_parts):
            for side in range(2):
                @pl.when(sends(side, 1))
                def _():
                    hop(a, side, 1, c).start()

    def arrive(a, step):
        for c in range(gather_parts):
            for side in range(2):
                toward = 1 if side == 0 else -1

                @pl.when(gets(side, step))
                def _():
                    landed = full.at[a, at_rows(me - toward * step), part(c, gather_parts)]
                    remote(
                        landed, landed,
                        ss.at[a, side, step - 1, c], rs.at[a, side, step - 1, c], "tp",
                        jnp.where(me == 0, 1, me - 1),
                    ).wait_recv()

                if step < n - 1:
                    @pl.when(sends(side, step + 1))
                    def _():
                        hop(a, side, step + 1, c).start()

    def square(a, which, index):
        wide = full[a, at_rows(index), :].astype(f32)
        inverse = lax.rsqrt(jnp.mean(wide * wide, axis=-1, keepdims=True) + epsilon)
        inv[which, at_rows(index), :] = jnp.broadcast_to(inverse, (rows, HEAD))

    def arrive_square(a, which, step):
        arrive(a, step)
        for side in range(2):
            @pl.when(gets(side, step))
            def _():
                square(a, which, me - step if side == 0 else me + step)

    def multiply(a, right, out, which):
        tile = min(256, right.shape[1])

        @pl.loop(0, right.shape[1] // tile)
        def _(t):
            columns = pl.ds(pl.multiple_of(t * tile, tile), tile)
            product = jnp.dot(full[a], right[:, columns], preferred_element_type=f32)
            if which is not None:
                product = product * inv[which, :, :1]
            out[:, columns] = product.astype(bf16)

    def allowed(which):
        numbers = jnp.broadcast_to(docs[which : which + 1, :].astype(f32), (seq, seq))
        i = lax.broadcasted_iota(jnp.int32, (seq, seq), 0)
        j = lax.broadcasted_iota(jnp.int32, (seq, seq), 1)
        return (j <= i) & (numbers == numbers.T)

    def stack(ref, g):
        first = g * group
        return jnp.concatenate(
            [ref[:, (first + h) * HEAD : (first + h + 1) * HEAD] for h in range(group)], axis=0
        )

    def head(ref, g):
        return ref[:, g * HEAD : (g + 1) * HEAD]

    def probabilities(which, g):
        scores = contract_last(stack(q, g), head(k, g)) * scale
        pairs = allowed(which)
        scores = jnp.where(jnp.concatenate([pairs] * group, axis=0), scores, -jnp.inf)
        weights = jnp.exp(scores - jnp.max(scores, axis=-1, keepdims=True))
        return (weights / jnp.sum(weights, axis=-1, keepdims=True)).astype(bf16)

    def attend_back(g):
        weights = probs[g]
        wide = weights.astype(f32)
        stacked = stack(dm, g)
        dprobs = contract_last(stacked, head(v, g))
        inner = jnp.sum(wide * dprobs, axis=-1, keepdims=True)
        dscores = (wide * (dprobs - inner) * scale).astype(bf16)
        dqueries = jnp.dot(dscores, head(k, g), preferred_element_type=f32)
        inverse = inv[0, :, :]
        for h in range(group):
            columns = slice((g * group + h) * HEAD, (g * group + h + 1) * HEAD)
            one = dqueries[h * seq : (h + 1) * seq]
            dq[:, columns] = one.astype(bf16)
            aq[mine, :, columns] = (one * inverse).astype(bf16)
        columns = slice(g * HEAD, (g + 1) * HEAD)
        dkeys = contract_first(dscores, stack(q, g))
        dk[:, columns] = dkeys.astype(bf16)
        ak[mine, :, columns] = (dkeys * inverse).astype(bf16)
        dvalues = contract_first(weights, stacked)
        dv[:, columns] = dvalues.astype(bf16)
        av[mine, :, columns] = (dvalues * inverse).astype(bf16)

    def copy(a, side, dest, c, first):
        toward = 1 if side == 0 else -1
        columns = part(c, sum_parts)
        target = slots.at[a, side, dest, :, columns]
        source = sums.at[a, at_rows(dest), columns] if first else target
        return remote(
            source, target, ts.at[a, side, dest, c], tr.at[a, side, dest, c], "tp", me + toward
        )

    def landed(a, side, dest, c):
        slot = slots.at[a, side, dest, :, part(c, sum_parts)]
        remote(
            slot, slot, ts.at[a, side, dest, c], tr.at[a, side, dest, c], "tp",
            jnp.where(me == 0, 1, me - 1),
        ).wait_recv()

    def roles(side, dest):
        if side == 0:
            return me == 0, (me > 0) & (me < dest)
        return me == n - 1, (me < n - 1) & (me > dest)

    def route(side, turn):
        return n - 1 - turn if side == 0 else turn

    def first_send(a, turn, c):
        for side in range(2):
            dest = route(side, turn)

            @pl.when(roles(side, dest)[0])
            def _():
                copy(a, side, dest, c, True).start()

    def pass_on(a, turn, c):
        columns = part(c, sum_parts)
        for side in range(2):
            dest = route(side, turn)

            @pl.when(roles(side, dest)[1])
            def _():
                landed(a, side, dest, c)
                slots[a, side, dest, :, columns] = (
                    slots[a, side, dest, :, columns].astype(f32)
                    + sums[a, at_rows(dest), columns].astype(f32)
                ).astype(bf16)
                copy(a, side, dest, c, False).start()

    def collect(a, c, base):
        columns = part(c, sum_parts)
        mine_sum = sums[a, at_rows(me), columns].astype(f32)
        total[:, columns] = mine_sum if base is None else mine_sum + base[:, columns].astype(f32)
        for side in range(2):
            @pl.when(me > 0 if side == 0 else me < n - 1)
            def _():
                landed(a, side, me, c)
                total[:, columns] += slots[a, side, me, :, columns].astype(f32)

    def spread(a, pairs):
        tile = min(256, width // sum_parts)
        for c in range(sum_parts):
            base = c * (width // sum_parts)

            @pl.loop(0, width // sum_parts // tile)
            def _(t):
                features = pl.ds(pl.multiple_of(base + t * tile, tile), tile)
                acc = None
                for left, right in pairs:
                    term = contract_last(left[...], right[features, :])
                    acc = term if acc is None else acc + term
                sums[a, :, features] = acc.astype(bf16)

            first_send(a, 0, c)
        for turn in range(1, n - 1):
            for c in range(sum_parts):
                first_send(a, turn, c)

    start(0)
    for a in range(3):
        full[a, at_rows(me), :] = own[a][...]
    square(0, 0, me)
    square(2, 1, me)
    for step in range(1, n):
        arrive_square(0, 0, step)
        if step == max(n - 2, 1):
            start(1)
    trades = []

    def trade(i, source, target):
        for offset in range(1, copies):
            other = lax.rem(mine + offset, copies)
            one = remote(
                source(other), target, dss.at[offset, i], drs.at[offset, i], "dp", other
            )
            one.start()
            trades.append(one)

    trade(
        0, lambda other: full.at[0, :, pl.ds(pl.multiple_of(other * piece, piece), piece)],
        ncols.at[mine],
    )
    ncols[mine] = full[0, :, pl.ds(pl.multiple_of(mine * piece, piece), piece)]
    for load in loads:
        load.wait()
    multiply(0, vq, q, 0)
    arrive(1, 1)
    multiply(0, vk, k, 0)
    multiply(0, vv, v, 0)
    for g in range(kv_local):
        probs[g] = probabilities(1, g)
    for step in range(2, n):
        arrive(1, step)
        if step == max(n - 2, 1):
            start(2)
    multiply(1, vo, dm, None)
    for g in range(kv_local):
        attend_back(g)
    for i, target in enumerate((aq, ak, av)):
        trade(i + 1, lambda other: target.at[mine], target.at[mine])
    arrive_square(2, 1, 1)
    spread(0, ((dq, vq), (dk, vk), (dv, vv)))
    for step in range(2, n):
        arrive_square(2, 1, step)

    multiply(2, vq, q, 1)
    multiply(2, vk, k, 1)
    multiply(2, vv, v, 1)
    for g in range(kv_local):
        heads = jnp.dot(
            probabilities(0, g), head(v, g), preferred_element_type=f32
        ).astype(bf16)
        for h in range(group):
            columns = slice((g * group + h) * HEAD, (g * group + h + 1) * HEAD)
            mixed[:, columns] = heads[h * seq : (h + 1) * seq]
    spread(1, ((mixed, vo),))

    handoffs = []
    for turn in range(n - 1):
        for c in range(sum_parts):
            pass_on(0, turn, c)
    for c in range(sum_parts):
        collect(0, c, None)
    inverse = inv[0, at_rows(me), :1]
    scaled = stash[...].astype(f32) * inverse
    centred = total[...] - scaled * jnp.mean(total[...] * scaled, axis=-1, keepdims=True)
    outgoing[0] = (grad[...].astype(f32) + inverse * centred).astype(bf16)
    for c in range(sum_parts):
        columns = part(c, sum_parts)
        handoff = remote(
            outgoing.at[0, :, columns], grad_out.at[:, columns], hs.at[0, c], hr.at[0, c],
            "pp", behind,
        )
        handoff.start()
        handoffs.append(handoff)

    for turn in range(n - 1):
        for c in range(sum_parts):
            pass_on(1, turn, c)
    for c in range(sum_parts):
        columns = part(c, sum_parts)
        collect(1, c, act)
        outgoing[1, :, columns] = total[:, columns].astype(bf16)
        handoff = remote(
            outgoing.at[1, :, columns], act_out.at[:, columns], hs.at[1, c], hr.at[1, c],
            "pp", ahead,
        )
        handoff.start()
        handoffs.append(handoff)

    for a in range(3):
        for step in range(1, n):
            for c in range(gather_parts):
                for side in range(2):
                    @pl.when(sends(side, step))
                    def _():
                        hop(a, side, step, c).wait_send()
    for a in range(2):
        for turn in range(n - 1):
            for c in range(sum_parts):
                for side in range(2):
                    dest = route(side, turn)
                    first, middle = roles(side, dest)

                    @pl.when(first | middle)
                    def _():
                        copy(a, side, dest, c, False).wait_send()
    for one in trades + handoffs:
        one.wait()


def section_call(n, copies, stages, stash, grad, act, docs, wq, wk, wv, wo):
    rows, width = act.shape
    seq = rows * n
    gather_parts, sum_parts = chunking(rows, width)
    vmem = pl.BlockSpec(memory_space=pltpu.VMEM)
    anywhere = pl.BlockSpec(memory_space=pl.ANY)
    heads = wk.shape[1] // HEAD
    group = wq.shape[1] // wk.shape[1]
    shapes = [(rows, width), (rows, width), (copies, seq, width // copies)]
    shapes += [(copies, seq, w.shape[1]) for w in (wq, wk, wv)]
    sem = pltpu.SemaphoreType.DMA
    flops = 2 * seq * width * (3 * wq.shape[1] + 3 * wk.shape[1] + 3 * wv.shape[1] + wo.shape[1])
    return pl.pallas_call(
        functools.partial(section_kernel, n, copies, stages, gather_parts, sum_parts),
        out_shape=[jax.ShapeDtypeStruct(shape, bf16) for shape in shapes],
        in_specs=[vmem] * 4 + [anywhere] * 4,
        out_specs=[vmem] * len(shapes),
        scratch_shapes=[
            pltpu.VMEM((3, seq, width), bf16),
            pltpu.VMEM((2, seq, HEAD), f32),
        ]
        + [pltpu.VMEM(w.shape, bf16) for w in (wq, wk, wv, wo)]
        + [pltpu.VMEM((seq, w.shape[1]), bf16) for w in (wq, wk, wv, wo, wo)]
        + [pltpu.VMEM((heads, group * seq, seq), bf16)]
        + [pltpu.VMEM((seq, w.shape[1]), bf16) for w in (wq, wk, wv)]
        + [
            pltpu.VMEM((2, seq, width), bf16),
            pltpu.VMEM((2, 2, n, rows, width), bf16),
            pltpu.VMEM((rows, width), f32),
            pltpu.VMEM((2, rows, width), bf16),
            sem((4,)),
            sem((3, 2, n, gather_parts)), sem((3, 2, n, gather_parts)),
            sem((2, 2, n, sum_parts)), sem((2, 2, n, sum_parts)),
            sem((copies, 4)), sem((copies, 4)),
            sem((2, sum_parts)), sem((2, sum_parts)),
        ],
        compiler_params=pltpu.CompilerParams(
            collective_id=0, has_side_effects=True, vmem_limit_bytes=VMEM_LIMIT
        ),
        cost_estimate=pl.CostEstimate(
            flops=flops, bytes_accessed=30_000_000, transcendentals=0
        ),
    )(stash, grad, act, docs, wq, wk, wv, wo)


def weights_kernel(ncols, aq, ak, av, gq, gk, gv):
    left = ncols[...].reshape(-1, ncols.shape[2])
    for right, out in ((aq, gq), (ak, gk), (av, gv)):
        out[...] = contract_first(left, right[...].reshape(-1, right.shape[2]))


def weights_call(ncols, aq, ak, av):
    copies, seq, piece = ncols.shape
    tile = min(256, piece)
    whole = [pl.BlockSpec(g.shape, lambda t: (0, 0, 0)) for g in (aq, ak, av)]
    outs = [jax.ShapeDtypeStruct((piece, g.shape[2]), f32) for g in (aq, ak, av)]
    return pl.pallas_call(
        weights_kernel,
        grid=(piece // tile,),
        out_shape=outs,
        in_specs=[pl.BlockSpec((copies, seq, tile), lambda t: (0, 0, t))] + whole,
        out_specs=[pl.BlockSpec((tile, o.shape[1]), lambda t: (t, 0)) for o in outs],
        compiler_params=pltpu.CompilerParams(vmem_limit_bytes=40 * 1024 * 1024),
        cost_estimate=pl.CostEstimate(
            flops=2 * copies * seq * piece * sum(o.shape[1] for o in outs),
            bytes_accessed=4 * piece * sum(o.shape[1] for o in outs),
            transcendentals=0,
        ),
    )(ncols, aq, ak, av)


def body(act_in, stash_in, grad_in, doc_ids, query_weight, key_weight, value_weight, out_weight):
    n, copies, stages = (lax.axis_size(axis) for axis in ("tp", "dp", "pp"))
    act_out, grad_out, ncols, aq, ak, av = section_call(
        n, copies, stages, stash_in[0, 0], grad_in[0, 0], act_in[0, 0], doc_ids[0, 0],
        query_weight[0], key_weight[0], value_weight[0], out_weight[0],
    )
    grads = (grad[None] for grad in weights_call(ncols, aq, ak, av))
    return (act_out[None, None], grad_out[None, None], *grads)


def solution(mesh):
    placed = (
        P("pp", "dp", "tp", None),
        P("pp", "dp", "tp", None),
        P("pp", "dp", "tp", None),
        P("pp", "dp", None, None),
        P("pp", None, "tp"),
        P("pp", None, "tp"),
        P("pp", None, "tp"),
        P("pp", None, "tp"),
    )
    return jax.shard_map(
        body,
        mesh=mesh,
        in_specs=placed,
        out_specs=(
            P("pp", "dp", "tp", None),
            P("pp", "dp", "tp", None),
            P("pp", "dp", "tp"),
            P("pp", "dp", "tp"),
            P("pp", "dp", "tp"),
        ),
        check_vma=False,
    )
```

time: 144 us -> 138 us (0.958)
  Pallas kernels: 110 us -> 131 us
  matrix products: 16.7 us -> 0 us
  starting transfers between devices: 8.48 us -> 0 us
  other arithmetic: 1.78 us -> 0 us
    pallas_call x3 -> x2, Pallas kernels: 110 us -> 131 us  [the longest x1 125 us: section_call(): pl.pallas_call(functools.partial(section_kernel, n, copies, stages, gathe...]
    dot_general x10 -> x0, matrix products: 16 us -> none  [the longest x4 14.4 us: contract_last(): lax.dot_general(left_side, right_side, (((1,), (1,)), ((), ())), preferre...]
    ppermute x2 -> x0, starting transfers between devices: 8.48 us -> none  [from_behind(): return lax.ppermute(value, axis, pairs)]
    unnamed x24 -> x14, local copies, waits for them, and re-layouts: 2.22 us -> 5.48 us
    reshape x9 -> x0, local copies, waits for them, and re-layouts: 2.8 us -> none  [the longest x2 1.29 us: split_heads(): queries.reshape(length, kv_local, group_size, HEAD)]
  transfers between devices with their start and end apart: 2 -> 0, of which waited for: 0 -> 0; matrix products, arithmetic and copies ran while one was open for 0% -> 0% of each run, Pallas kernels for 5% -> 0%
where the time goes in v1:
time: 138 us; the launch traced here: 137 us
  Pallas kernels  131 us (95%)
  local copies, waits for them, and re-layouts  5.48 us (4%)
    pallas_call x1, Pallas kernels, section_call(): pl.pallas_call(functools.partial(section_kernel, n, copies, stages, gathe...  125 us
    pallas_call x1, Pallas kernels, weights_call(): pl.pallas_call(weights_kernel, grid=(piece // tile,), out_shape=outs, in_...  6.32 us
    unnamed x14, local copies, waits for them, and re-layouts  5.48 us

profile of v1, /device:TPU:1, one launch (start us, length us, event | category | flops | bytes accessed | tf_op | source)
XLA Modules:
  0.0 137.2 jit_solution(6304427549581892940)
XLA Ops:
  0.6 124.7 %shard_map.119 = (bf16[32,4096]{1,0:T(8,128)(2,1)}, bf16[32,4096]{1,0:T(8,128)(2,1)}, bf16[2,128,2048]{2,1,0:T(8,128)(2,1)}, bf16[2,128,1024]{2,1,0:T(8,128)(2,1...) custom-call(bf16[32,4096]{1,0:T(8,128)(2,1)} %bitcast.19, bf16[32,4096]{1,0:T(8,128)(2,1)} %bitcast.20, ...), custom_call_target="tpu_custom_call" | custom-call | flops 5905580032 | bytes 30000000 | tf_op jit(solution)/shard_map/pallas_call | solution.py:404
  125.3 0.0 copy-start
  125.3 1.2 copy-done
  126.6 0.0 copy-start.1
  126.6 1.0 copy-done.1
  127.6 0.0 copy-start.2
  127.6 0.9 copy-done.2
  128.5 0.0 copy-start.3
  128.5 0.9 copy-done.3
  129.4 0.0 copy-start.5
  129.4 0.0 copy-start.4
  129.4 6.3 %shard_map.120 = (f32[2048,1024]{1,0:T(8,128)}, f32[2048,256]{1,0:T(8,128)}, f32[2048,256]{1,0:T(8,128)}) custom-call(bf16[2,128,2048]{2,1,0:T(8,128)(2,1)S(1)} %copy-done, bf16[2,128,1024]{2,1,0:T(8,128)(2,1)S(1)} %copy-done.1, bf16[2,128,256]{2,1,0:T(8,128)(2,1)S(1)} %copy-done.2, bf16[2,128,256]{2,1,0:T(8,128)(2,1)S(1)} %copy-done.3), custom_call_target="tpu_custom_call" | custom-call | flops 1610612736 | bytes 12582912 | tf_op jit(solution)/shard_map/pallas_call | solution.py:448
  135.7 0.0 copy-done.5
  135.7 0.7 copy.15
  136.4 0.0 copy-done.4
  136.4 0.7 copy.16
Async XLA Ops:
  125.3 1.2 copy-start
  126.6 1.0 copy-start.1
  127.6 0.9 copy-start.2
  128.5 0.9 copy-start.3
  129.4 6.3 %copy-start.5 = (bf16[32,4096]{1,0:T(8,128)(2,1)S(1)}, bf16[32,4096]{1,0:T(8,128)(2,1)}, u32[]{:S(2)}) copy-start(bf16[32,4096]{1,0:T(8,128)(2,1)} %get-tuple-element.14) | copy-start | bytes 786436
  129.4 7.0 %copy-start.4 = (bf16[32,4096]{1,0:T(8,128)(2,1)S(1)}, bf16[32,4096]{1,0:T(8,128)(2,1)}, u32[]{:S(2)}) copy-start(bf16[32,4096]{1,0:T(8,128)(2,1)} %get-tuple-element.15) | copy-start | bytes 786436

commit v2 on v1

--- a/solution.py
+++ b/solution.py
@@ -233,19 +233,29 @@
             def _():
                 copy(a, side, dest, c, True).start()
 
-    def pass_on(a, turn, c):
-        columns = part(c, sum_parts)
-        for side in range(2):
-            dest = route(side, turn)
-
-            @pl.when(roles(side, dest)[1])
+    near = jnp.where(2 * me < n, 0, 1)
+
+    def pass_on(a, turn):
+        for side in (near, 1 - near):
+            toward = 1 - 2 * side
+            dest = jnp.where(side == 0, n - 1 - turn, turn)
+            upward = (side == 0) & (me > 0) & (me < dest)
+            downward = (side == 1) & (me < n - 1) & (me > dest)
+
+            @pl.when(upward | downward)
             def _():
-                landed(a, side, dest, c)
-                slots[a, side, dest, :, columns] = (
-                    slots[a, side, dest, :, columns].astype(f32)
-                    + sums[a, at_rows(dest), columns].astype(f32)
-                ).astype(bf16)
-                copy(a, side, dest, c, False).start()
+                for c in range(sum_parts):
+                    columns = part(c, sum_parts)
+                    landed(a, side, dest, c)
+                    slots[a, side, dest, :, columns] = (
+                        slots[a, side, dest, :, columns].astype(f32)
+                        + sums[a, at_rows(dest), columns].astype(f32)
+                    ).astype(bf16)
+                    slot = slots.at[a, side, dest, :, columns]
+                    remote(
+                        slot, slot, ts.at[a, side, dest, c], tr.at[a, side, dest, c], "tp",
+                        me + toward,
+                    ).start()
 
     def collect(a, c, base):
         columns = part(c, sum_parts)
@@ -337,8 +347,7 @@
 
     handoffs = []
     for turn in range(n - 1):
-        for c in range(sum_parts):
-            pass_on(0, turn, c)
+        pass_on(0, turn)
     for c in range(sum_parts):
         collect(0, c, None)
     inverse = inv[0, at_rows(me), :1]
@@ -355,8 +364,7 @@
         handoffs.append(handoff)
 
     for turn in range(n - 1):
-        for c in range(sum_parts):
-            pass_on(1, turn, c)
+        pass_on(1, turn)
     for c in range(sum_parts):
         columns = part(c, sum_parts)
         collect(1, c, act)
@@ -434,40 +442,50 @@
     )(stash, grad, act, docs, wq, wk, wv, wo)
 
 
-def weights_kernel(ncols, aq, ak, av, gq, gk, gv):
+def weights_kernel(ncols, aq, ak, av, act_sent, grad_sent, gq, gk, gv, act_out, grad_out):
     left = ncols[...].reshape(-1, ncols.shape[2])
     for right, out in ((aq, gq), (ak, gk), (av, gv)):
         out[...] = contract_first(left, right[...].reshape(-1, right.shape[2]))
-
-
-def weights_call(ncols, aq, ak, av):
+    act_out[...] = act_sent[...]
+    grad_out[...] = grad_sent[...]
+
+
+def weights_call(ncols, aq, ak, av, act_sent, grad_sent):
     copies, seq, piece = ncols.shape
-    tile = min(256, piece)
+    rows, width = act_sent.shape
+    steps = max(1, piece // 256)
+    tile = piece // steps
     whole = [pl.BlockSpec(g.shape, lambda t: (0, 0, 0)) for g in (aq, ak, av)]
+    sent = [pl.BlockSpec((rows, width // steps), lambda t: (0, t))] * 2
     outs = [jax.ShapeDtypeStruct((piece, g.shape[2]), f32) for g in (aq, ak, av)]
     return pl.pallas_call(
         weights_kernel,
-        grid=(piece // tile,),
-        out_shape=outs,
-        in_specs=[pl.BlockSpec((copies, seq, tile), lambda t: (0, 0, t))] + whole,
-        out_specs=[pl.BlockSpec((tile, o.shape[1]), lambda t: (t, 0)) for o in outs],
-        compiler_params=pltpu.CompilerParams(vmem_limit_bytes=40 * 1024 * 1024),
+        grid=(steps,),
+        out_shape=outs + [jax.ShapeDtypeStruct((rows, width), bf16)] * 2,
+        in_specs=[pl.BlockSpec((copies, seq, tile), lambda t: (0, 0, t))] + whole + sent,
+        out_specs=[pl.BlockSpec((tile, o.shape[1]), lambda t: (t, 0)) for o in outs] + sent,
+        compiler_params=pltpu.CompilerParams(vmem_limit_bytes=VMEM_LIMIT),
         cost_estimate=pl.CostEstimate(
             flops=2 * copies * seq * piece * sum(o.shape[1] for o in outs),
             bytes_accessed=4 * piece * sum(o.shape[1] for o in outs),
             transcendentals=0,
         ),
-    )(ncols, aq, ak, av)
+    )(ncols, aq, ak, av, act_sent, grad_sent)
 
 
 def body(act_in, stash_in, grad_in, doc_ids, query_weight, key_weight, value_weight, out_weight):
     n, copies, stages = (lax.axis_size(axis) for axis in ("tp", "dp", "pp"))
-    act_out, grad_out, ncols, aq, ak, av = section_call(
+    act_sent, grad_sent, ncols, aq, ak, av = section_call(
         n, copies, stages, stash_in[0, 0], grad_in[0, 0], act_in[0, 0], doc_ids[0, 0],
         query_weight[0], key_weight[0], value_weight[0], out_weight[0],
     )
-    grads = (grad[None] for grad in weights_call(ncols, aq, ak, av))
-    return (act_out[None, None], grad_out[None, None], *grads)
+    grad_query, grad_key, grad_value, act_out, grad_out = weights_call(
+        ncols, aq, ak, av, act_sent, grad_sent
+    )
+    return (
+        act_out[None, None], grad_out[None, None],
+        grad_query[None], grad_key[None], grad_value[None],
+    )
 
 
 def solution(mesh):

time: 138 us -> 99.7 us (0.72)
  Pallas kernels: 131 us -> 98.6 us
  local copies, waits for them, and re-layouts: 5.48 us -> 0 us
    pallas_call x1, Pallas kernels: 125 us -> 90.1 us  [section_call(): pl.pallas_call(functools.partial(section_kernel, n, copies, stages, gathe...]
    unnamed x14 -> x0, local copies, waits for them, and re-layouts: 5.48 us -> none
    pallas_call x1, Pallas kernels: 6.32 us -> 8.45 us  [weights_call(): pl.pallas_call(weights_kernel, grid=(steps,), out_shape=outs + [jax.Shape...]
where the time goes in v2:
time: 99.7 us; the launch traced here: 99.2 us
  Pallas kernels  98.6 us (99%)
    pallas_call x1, Pallas kernels, section_call(): pl.pallas_call(functools.partial(section_kernel, n, copies, stages, gathe...  90.1 us
    pallas_call x1, Pallas kernels, weights_call(): pl.pallas_call(weights_kernel, grid=(steps,), out_shape=outs + [jax.Shape...  8.45 us

profile of v2, /device:TPU:1, one launch (start us, length us, event | category | flops | bytes accessed | tf_op | source)
XLA Modules:
  0.0 99.2 jit_solution(7018607295864773457)
XLA Ops:
  0.6 90.1 %shard_map.119 = (bf16[32,4096]{1,0:T(8,128)(2,1)}, bf16[32,4096]{1,0:T(8,128)(2,1)}, bf16[2,128,2048]{2,1,0:T(8,128)(2,1)}, bf16[2,128,1024]{2,1,0:T(8,128)(2,1...) custom-call(bf16[32,4096]{1,0:T(8,128)(2,1)} %bitcast.17, bf16[32,4096]{1,0:T(8,128)(2,1)} %bitcast.18, ...), custom_call_target="tpu_custom_call" | custom-call | flops 5905580032 | bytes 30000000 | tf_op jit(solution)/shard_map/pallas_call | solution.py:412
  90.8 8.4 %shard_map.120 = (f32[2048,1024]{1,0:T(8,128)}, f32[2048,256]{1,0:T(8,128)}, f32[2048,256]{1,0:T(8,128)}, bf16[32,4096]{1,0:T(8,128)(2,1)}, bf16[32,4096]{1,0:T(8,128)(2,1)}) custom-call(bf16[2,128,2048]{2,1,0:T(8,128)(2,1)} %get-tuple-element.16.ncols, bf16[2,128,1024]{2,1,0:T(8,128)(2,1)} %get-tuple-element.17.aq, ...), custom_call_target="tpu_custom_call" | custom-call | flops 1610612736 | bytes 12582912 | tf_op jit(solution)/shard_map/pallas_call | solution.py:461

commit v3 on v1

--- a/solution.py
+++ b/solution.py
@@ -11,7 +11,7 @@
 HEAD = 128
 epsilon = 1e-05
 MESH = pl.DeviceIdType.MESH
-VMEM_LIMIT = 62 * 1024 * 1024
+VMEM_LIMIT = 40 * 1024 * 1024
 bf16 = jnp.bfloat16
 f32 = jnp.float32
 
@@ -36,15 +36,15 @@
 
 
 def chunking(rows, width):
-    return (2, 4) if rows * width >= 32 * 4096 else (1, 1)
+    return (4, 4) if rows * width >= 32 * 4096 else (1, 1)
 
 
 def section_kernel(
     n, copies, stages, gather_parts, sum_parts,
     stash, grad, act, docs, wq, wk, wv, wo,
-    act_out, grad_out, ncols, aq, ak, av,
+    act_out, grad_out, wgq, wgk, wgv,
     full, inv, vq, vk, vv, vo, q, k, v, dm, mixed, probs, dq, dk, dv,
-    sums, slots, total, outgoing,
+    ncols, aq, ak, av, acc, sums, slots, total, outgoing,
     wsem, ss, rs, ts, tr, dss, drs, hs, hr,
 ):
     me = lax.axis_index("tp")
@@ -56,10 +56,14 @@
     kv_local = vk.shape[1] // HEAD
     group = vq.shape[1] // (kv_local * HEAD)
     scale = 1.0 / math.sqrt(HEAD)
-    own = (stash, grad, act)
+
+    def at_rows(index):
+        return pl.ds(pl.multiple_of(index * rows, rows), rows)
 
     loads = []
-    for i, (hbm, vmem) in enumerate(((wq, vq), (wk, vk), (wv, vv), (wo, vo))):
+    pairs = [(own, full.at[a, at_rows(me), :]) for a, own in enumerate((stash, grad, act))]
+    pairs += [(wq, vq), (wk, vk), (wv, vv), (wo, vo)]
+    for i, (hbm, vmem) in enumerate(pairs):
         load = pltpu.make_async_copy(hbm, vmem, wsem.at[i])
         load.start()
         loads.append(load)
@@ -83,9 +87,6 @@
     ends = jnp.where(me > 0, 1, 0) + jnp.where(me < n - 1, 1, 0)
     pl.semaphore_wait(barrier, ends + copies - 1 + 2)
 
-    def at_rows(index):
-        return pl.ds(pl.multiple_of(index * rows, rows), rows)
-
     def part(c, parts):
         return pl.ds(c * (width // parts), width // parts)
 
@@ -93,10 +94,9 @@
         toward = 1 if side == 0 else -1
         carried = me - toward * (step - 1)
         columns = part(c, gather_parts)
-        target = full.at[a, at_rows(carried), columns]
-        source = own[a].at[:, columns] if step == 1 else target
+        block = full.at[a, at_rows(carried), columns]
         return remote(
-            source, target, ss.at[a, side, step - 1, c], rs.at[a, side, step - 1, c],
+            block, block, ss.at[a, side, step - 1, c], rs.at[a, side, step - 1, c],
             "tp", me + toward,
         )
 
@@ -115,8 +115,8 @@
                 def _():
                     hop(a, side, 1, c).start()
 
-    def arrive(a, step):
-        for c in range(gather_parts):
+    def arrive(a, step, parts=None):
+        for c in range(gather_parts) if parts is None else parts:
             for side in range(2):
                 toward = 1 if side == 0 else -1
 
@@ -139,23 +139,31 @@
         inverse = lax.rsqrt(jnp.mean(wide * wide, axis=-1, keepdims=True) + epsilon)
         inv[which, at_rows(index), :] = jnp.broadcast_to(inverse, (rows, HEAD))
 
-    def arrive_square(a, which, step):
-        arrive(a, step)
+    def squares(a, which, step):
         for side in range(2):
             @pl.when(gets(side, step))
             def _():
                 square(a, which, me - step if side == 0 else me + step)
 
-    def multiply(a, right, out, which):
+    def multiply(a, right, out, which, c=None, kept=0):
         tile = min(256, right.shape[1])
+        features = slice(None) if c is None else part(c, gather_parts)
 
         @pl.loop(0, right.shape[1] // tile)
         def _(t):
             columns = pl.ds(pl.multiple_of(t * tile, tile), tile)
-            product = jnp.dot(full[a], right[:, columns], preferred_element_type=f32)
-            if which is not None:
-                product = product * inv[which, :, :1]
-            out[:, columns] = product.astype(bf16)
+            held = pl.ds(pl.multiple_of(kept + t * tile, tile), tile)
+            product = jnp.dot(
+                full[a, :, features], right[features, columns], preferred_element_type=f32
+            )
+            if c is not None and c > 0:
+                product = product + acc[:, held]
+            if c is None or c == gather_parts - 1:
+                if which is not None:
+                    product = product * inv[which, :, :1]
+                out[:, columns] = product.astype(bf16)
+            else:
+                acc[:, held] = product
 
     def allowed(which):
         numbers = jnp.broadcast_to(docs[which : which + 1, :].astype(f32), (seq, seq))
@@ -233,24 +241,40 @@
             def _():
                 copy(a, side, dest, c, True).start()
 
-    def pass_on(a, turn, c):
-        columns = part(c, sum_parts)
-        for side in range(2):
-            dest = route(side, turn)
-
-            @pl.when(roles(side, dest)[1])
-            def _():
+    near = jnp.where(2 * me < n, 0, 1)
+
+    def pass_on(a, turn, side):
+        toward = 1 - 2 * side
+        dest = jnp.where(side == 0, n - 1 - turn, turn)
+        upward = (side == 0) & (me > 0) & (me < dest)
+        downward = (side == 1) & (me < n - 1) & (me > dest)
+
+        @pl.when(upward | downward)
+        def _():
+            for c in range(sum_parts):
+                columns = part(c, sum_parts)
                 landed(a, side, dest, c)
                 slots[a, side, dest, :, columns] = (
                     slots[a, side, dest, :, columns].astype(f32)
                     + sums[a, at_rows(dest), columns].astype(f32)
                 ).astype(bf16)
-                copy(a, side, dest, c, False).start()
+                slot = slots.at[a, side, dest, :, columns]
+                remote(
+                    slot, slot, ts.at[a, side, dest, c], tr.at[a, side, dest, c], "tp",
+                    me + toward,
+                ).start()
+
+    def pass_all(a):
+        for side in (near, 1 - near):
+            for turn in range(n - 1):
+                pass_on(a, turn, side)
 
     def collect(a, c, base):
         columns = part(c, sum_parts)
         mine_sum = sums[a, at_rows(me), columns].astype(f32)
-        total[:, columns] = mine_sum if base is None else mine_sum + base[:, columns].astype(f32)
+        if base is not None:
+            mine_sum = mine_sum + full[base, at_rows(me), columns].astype(f32)
+        total[:, columns] = mine_sum
         for side in range(2):
             @pl.when(me > 0 if side == 0 else me < n - 1)
             def _():
@@ -276,13 +300,15 @@
             for c in range(sum_parts):
                 first_send(a, turn, c)
 
+    loads[0].wait()
     start(0)
-    for a in range(3):
-        full[a, at_rows(me), :] = own[a][...]
     square(0, 0, me)
+    loads[1].wait()
+    loads[2].wait()
     square(2, 1, me)
     for step in range(1, n):
-        arrive_square(0, 0, step)
+        arrive(0, step)
+        squares(0, 0, step)
         if step == max(n - 2, 1):
             start(1)
     trades = []
@@ -301,7 +327,7 @@
         ncols.at[mine],
     )
     ncols[mine] = full[0, :, pl.ds(pl.multiple_of(mine * piece, piece), piece)]
-    for load in loads:
+    for load in loads[3:]:
         load.wait()
     multiply(0, vq, q, 0)
     arrive(1, 1)
@@ -309,23 +335,30 @@
     multiply(0, vv, v, 0)
     for g in range(kv_local):
         probs[g] = probabilities(1, g)
-    for step in range(2, n):
+    for step in range(2, n - 1):
         arrive(1, step)
-        if step == max(n - 2, 1):
-            start(2)
-    multiply(1, vo, dm, None)
+    start(2)
+    for c in range(gather_parts):
+        if n > 2:
+            arrive(1, n - 1, (c,))
+        multiply(1, vo, dm, None, c)
     for g in range(kv_local):
         attend_back(g)
     for i, target in enumerate((aq, ak, av)):
         trade(i + 1, lambda other: target.at[mine], target.at[mine])
-    arrive_square(2, 1, 1)
     spread(0, ((dq, vq), (dk, vk), (dv, vv)))
-    for step in range(2, n):
-        arrive_square(2, 1, step)
-
-    multiply(2, vq, q, 1)
-    multiply(2, vk, k, 1)
-    multiply(2, vv, v, 1)
+
+    for step in range(1, n - 1):
+        arrive(2, step)
+        squares(2, 1, step)
+    for c in range(gather_parts):
+        arrive(2, n - 1, (c,))
+        if c == gather_parts - 1:
+            squares(2, 1, n - 1)
+        kept = 0
+        for right, out in ((vq, q), (vk, k), (vv, v)):
+            multiply(2, right, out, 1, c, kept)
+            kept += right.shape[1]
     for g in range(kv_local):
         heads = jnp.dot(
             probabilities(0, g), head(v, g), preferred_element_type=f32
@@ -335,16 +368,27 @@
             mixed[:, columns] = heads[h * seq : (h + 1) * seq]
     spread(1, ((mixed, vo),))
 
+    pass_all(0)
+    for one in trades:
+        one.wait()
+    tile = min(256, piece)
+
+    @pl.loop(0, piece // tile)
+    def _(t):
+        features = pl.ds(pl.multiple_of(t * tile, tile), tile)
+        left = ncols[:, :, features].reshape(copies * seq, tile)
+        for right, out in ((aq, wgq), (ak, wgk), (av, wgv)):
+            out[features, :] = contract_first(
+                left, right[...].reshape(copies * seq, right.shape[2])
+            )
+
     handoffs = []
-    for turn in range(n - 1):
-        for c in range(sum_parts):
-            pass_on(0, turn, c)
     for c in range(sum_parts):
         collect(0, c, None)
     inverse = inv[0, at_rows(me), :1]
-    scaled = stash[...].astype(f32) * inverse
+    scaled = full[0, at_rows(me), :].astype(f32) * inverse
     centred = total[...] - scaled * jnp.mean(total[...] * scaled, axis=-1, keepdims=True)
-    outgoing[0] = (grad[...].astype(f32) + inverse * centred).astype(bf16)
+    outgoing[0] = (full[1, at_rows(me), :].astype(f32) + inverse * centred).astype(bf16)
     for c in range(sum_parts):
         columns = part(c, sum_parts)
         handoff = remote(
@@ -354,12 +398,10 @@
         handoff.start()
         handoffs.append(handoff)
 
-    for turn in range(n - 1):
-        for c in range(sum_parts):
-            pass_on(1, turn, c)
+    pass_all(1)
     for c in range(sum_parts):
         columns = part(c, sum_parts)
-        collect(1, c, act)
+        collect(1, c, 2)
         outgoing[1, :, columns] = total[:, columns].astype(bf16)
         handoff = remote(
             outgoing.at[1, :, columns], act_out.at[:, columns], hs.at[1, c], hr.at[1, c],
@@ -385,8 +427,12 @@
                     @pl.when(first | middle)
                     def _():
                         copy(a, side, dest, c, False).wait_send()
-    for one in trades + handoffs:
+    for one in handoffs:
         one.wait()
+
+
+def pin(x):
+    return pltpu.with_memory_space_constraint(x, pltpu.HBM)
 
 
 def section_call(n, copies, stages, stash, grad, act, docs, wq, wk, wv, wo):
@@ -394,18 +440,20 @@
     seq = rows * n
     gather_parts, sum_parts = chunking(rows, width)
     vmem = pl.BlockSpec(memory_space=pltpu.VMEM)
-    anywhere = pl.BlockSpec(memory_space=pl.ANY)
+    hbm = pl.BlockSpec(memory_space=pltpu.HBM)
     heads = wk.shape[1] // HEAD
     group = wq.shape[1] // wk.shape[1]
-    shapes = [(rows, width), (rows, width), (copies, seq, width // copies)]
-    shapes += [(copies, seq, w.shape[1]) for w in (wq, wk, wv)]
+    piece = width // copies
+    outs = [jax.ShapeDtypeStruct((rows, width), bf16)] * 2
+    outs += [jax.ShapeDtypeStruct((piece, w.shape[1]), f32) for w in (wq, wk, wv)]
+    held = wq.shape[1] + wk.shape[1] + wv.shape[1]
     sem = pltpu.SemaphoreType.DMA
     flops = 2 * seq * width * (3 * wq.shape[1] + 3 * wk.shape[1] + 3 * wv.shape[1] + wo.shape[1])
     return pl.pallas_call(
         functools.partial(section_kernel, n, copies, stages, gather_parts, sum_parts),
-        out_shape=[jax.ShapeDtypeStruct(shape, bf16) for shape in shapes],
-        in_specs=[vmem] * 4 + [anywhere] * 4,
-        out_specs=[vmem] * len(shapes),
+        out_shape=outs,
+        in_specs=[hbm] * 3 + [vmem] + [hbm] * 4,
+        out_specs=[vmem] * len(outs),
         scratch_shapes=[
             pltpu.VMEM((3, seq, width), bf16),
             pltpu.VMEM((2, seq, HEAD), f32),
@@ -414,12 +462,15 @@
         + [pltpu.VMEM((seq, w.shape[1]), bf16) for w in (wq, wk, wv, wo, wo)]
         + [pltpu.VMEM((heads, group * seq, seq), bf16)]
         + [pltpu.VMEM((seq, w.shape[1]), bf16) for w in (wq, wk, wv)]
+        + [pltpu.VMEM((copies, seq, piece), bf16)]
+        + [pltpu.VMEM((copies, seq, w.shape[1]), bf16) for w in (wq, wk, wv)]
         + [
+            pltpu.VMEM((seq, held), f32),
             pltpu.VMEM((2, seq, width), bf16),
             pltpu.VMEM((2, 2, n, rows, width), bf16),
             pltpu.VMEM((rows, width), f32),
             pltpu.VMEM((2, rows, width), bf16),
-            sem((4,)),
+            sem((7,)),
             sem((3, 2, n, gather_parts)), sem((3, 2, n, gather_parts)),
             sem((2, 2, n, sum_parts)), sem((2, 2, n, sum_parts)),
             sem((copies, 4)), sem((copies, 4)),
@@ -431,43 +482,52 @@
         cost_estimate=pl.CostEstimate(
             flops=flops, bytes_accessed=30_000_000, transcendentals=0
         ),
-    )(stash, grad, act, docs, wq, wk, wv, wo)
-
-
-def weights_kernel(ncols, aq, ak, av, gq, gk, gv):
-    left = ncols[...].reshape(-1, ncols.shape[2])
-    for right, out in ((aq, gq), (ak, gk), (av, gv)):
-        out[...] = contract_first(left, right[...].reshape(-1, right.shape[2]))
-
-
-def weights_call(ncols, aq, ak, av):
-    copies, seq, piece = ncols.shape
-    tile = min(256, piece)
-    whole = [pl.BlockSpec(g.shape, lambda t: (0, 0, 0)) for g in (aq, ak, av)]
-    outs = [jax.ShapeDtypeStruct((piece, g.shape[2]), f32) for g in (aq, ak, av)]
+    )(*(pin(x) for x in (stash, grad, act)), docs, *(pin(x) for x in (wq, wk, wv, wo)))
+
+
+def store_kernel(*refs):
+    count = (len(refs) - 1) // 2
+    sems = refs[-1]
+    copies = []
+    for i, (source, target) in enumerate(zip(refs[:count], refs[count:-1])):
+        pieces = max(1, source.shape[0] // 512)
+        size = source.shape[0] // pieces
+        for p in range(pieces):
+            where = pl.ds(p * size, size)
+            one = pltpu.make_async_copy(source.at[where], target.at[where], sems.at[i, p])
+            one.start()
+            copies.append(one)
+    for one in copies:
+        one.wait()
+
+
+def store_call(*arrays):
+    pieces = max(1, max(a.shape[0] for a in arrays) // 512)
     return pl.pallas_call(
-        weights_kernel,
-        grid=(piece // tile,),
-        out_shape=outs,
-        in_specs=[pl.BlockSpec((copies, seq, tile), lambda t: (0, 0, t))] + whole,
-        out_specs=[pl.BlockSpec((tile, o.shape[1]), lambda t: (t, 0)) for o in outs],
-        compiler_params=pltpu.CompilerParams(vmem_limit_bytes=40 * 1024 * 1024),
+        store_kernel,
+        out_shape=[jax.ShapeDtypeStruct(a.shape, a.dtype) for a in arrays],
+        in_specs=[pl.BlockSpec(memory_space=pltpu.VMEM)] * len(arrays),
+        out_specs=[pl.BlockSpec(memory_space=pltpu.HBM)] * len(arrays),
+        scratch_shapes=[pltpu.SemaphoreType.DMA((len(arrays), pieces))],
+        compiler_params=pltpu.CompilerParams(vmem_limit_bytes=20 * 1024 * 1024),
         cost_estimate=pl.CostEstimate(
-            flops=2 * copies * seq * piece * sum(o.shape[1] for o in outs),
-            bytes_accessed=4 * piece * sum(o.shape[1] for o in outs),
+            flops=10_000_000, bytes_accessed=sum(2 * a.size * a.dtype.itemsize for a in arrays),
             transcendentals=0,
         ),
-    )(ncols, aq, ak, av)
+    )(*arrays)
 
 
 def body(act_in, stash_in, grad_in, doc_ids, query_weight, key_weight, value_weight, out_weight):
     n, copies, stages = (lax.axis_size(axis) for axis in ("tp", "dp", "pp"))
-    act_out, grad_out, ncols, aq, ak, av = section_call(
+    made = section_call(
         n, copies, stages, stash_in[0, 0], grad_in[0, 0], act_in[0, 0], doc_ids[0, 0],
         query_weight[0], key_weight[0], value_weight[0], out_weight[0],
     )
-    grads = (grad[None] for grad in weights_call(ncols, aq, ak, av))
-    return (act_out[None, None], grad_out[None, None], *grads)
+    act_out, grad_out, grad_query, grad_key, grad_value = store_call(*made)
+    return (
+        act_out[None, None], grad_out[None, None],
+        grad_query[None], grad_key[None], grad_value[None],
+    )
 
 
 def solution(mesh):

time: 138 us -> 92.7 us (0.67)
  Pallas kernels: 131 us -> 91.1 us
  local copies, waits for them, and re-layouts: 5.48 us -> 0.67 us
    pallas_call x1, Pallas kernels: 125 us -> 86.2 us  [section_call(): pl.pallas_call(functools.partial(section_kernel, n, copies, stages, gathe...]
    unnamed x14 -> x2, local copies, waits for them, and re-layouts: 5.48 us -> 0.67 us
    pallas_call x1, Pallas kernels: 6.32 us -> 4.89 us  [store_call(): pl.pallas_call(store_kernel, out_shape=[jax.ShapeDtypeStruct(a.shape, a.d...]
where the time goes in v3:
time: 92.7 us; the launch traced here: 92.4 us
  Pallas kernels  91.1 us (98%)
    pallas_call x1, Pallas kernels, section_call(): pl.pallas_call(functools.partial(section_kernel, n, copies, stages, gathe...  86.2 us
    pallas_call x1, Pallas kernels, store_call(): pl.pallas_call(store_kernel, out_shape=[jax.ShapeDtypeStruct(a.shape, a.d...  4.89 us

profile of v3, /device:TPU:1, one launch (start us, length us, event | category | flops | bytes accessed | tf_op | source)
XLA Modules:
  0.0 92.4 jit_solution(1123563448640274808)
XLA Ops:
  0.6 0.0 copy-start
  0.6 0.7 copy-done
  1.3 86.2 %shard_map.119 = (bf16[32,4096]{1,0:T(8,128)(2,1)S(1)}, bf16[32,4096]{1,0:T(8,128)(2,1)S(1)}, f32[2048,1024]{1,0:T(8,128)S(1)}, f32[2048,256]{1,0:T(8,128)S(1)}, f32[2048,256]{1,0:T(8,128)S(1)}) custom-call(bf16[32,4096]{1,0:T(8,128)(2,1)} %bitcast.21, bf16[32,4096]{1,0:T(8,128)(2,1)} %bitcast.22, bf16[32,4096]{1,0:T(8,128)(2,1)} %bitcast.23, ...), custom_call_target="tpu_custom_call" | custom-call | flops 5905580032 | bytes 30000000 | tf_op jit(solution)/shard_map/pallas_call | solution.py:452
  87.5 4.9 %shard_map.120 = (bf16[32,4096]{1,0:T(8,128)(2,1)}, bf16[32,4096]{1,0:T(8,128)(2,1)}, f32[2048,1024]{1,0:T(8,128)}, f32[2048,256]{1,0:T(8,128)}, f32[2048,256]{1,0:T(8,128)}) custom-call(bf16[32,4096]{1,0:T(8,128)(2,1)S(1)} %get-tuple-element.15.refs_0_, bf16[32,4096]{1,0:T(8,128)(2,1)S(1)} %get-tuple-element.16.refs_1_, ...), custom_call_target="tpu_custom_call" | custom-call | flops 10000000 | bytes 26214400 | tf_op jit(solution)/shard_map/pallas_call | solution.py:506
Async XLA Ops:
  0.6 0.7 copy-start

commit v4 on v3

--- a/solution.py
+++ b/solution.py
@@ -36,16 +36,22 @@
 
 
 def chunking(rows, width):
-    return (4, 4) if rows * width >= 32 * 4096 else (1, 1)
+    if rows * width < 32 * 4096:
+        return 1, ((width,), (width,))
+    eighth = width // 8
+    return 4, (
+        tuple(eighth * k for k in (1, 1, 2, 2, 2)),
+        tuple(eighth * k for k in (1, 2, 2, 1, 1, 1)),
+    )
 
 
 def section_kernel(
-    n, copies, stages, gather_parts, sum_parts,
-    stash, grad, act, docs, wq, wk, wv, wo,
+    n, copies, stages, gather_parts, cuts,
+    stash, grad, act, numbers, wq, wk, wv, wo,
     act_out, grad_out, wgq, wgk, wgv,
-    full, inv, vq, vk, vv, vo, q, k, v, dm, mixed, probs, dq, dk, dv,
+    docs, full, inv, vq, vk, vv, vo, q, k, v, dm, mixed, probs, dq, dk, dv,
     ncols, aq, ak, av, acc, sums, slots, total, outgoing,
-    wsem, ss, rs, ts, tr, dss, drs, hs, hr,
+    wsem, ss, rs, ts, tr_back, tr_ahead, dss, drs, hs, hr,
 ):
     me = lax.axis_index("tp")
     mine = lax.axis_index("dp")
@@ -62,7 +68,7 @@
 
     loads = []
     pairs = [(own, full.at[a, at_rows(me), :]) for a, own in enumerate((stash, grad, act))]
-    pairs += [(wq, vq), (wk, vk), (wv, vv), (wo, vo)]
+    pairs += [(wq, vq), (wk, vk), (wv, vv), (wo, vo), (numbers, docs)]
     for i, (hbm, vmem) in enumerate(pairs):
         load = pltpu.make_async_copy(hbm, vmem, wsem.at[i])
         load.start()
@@ -87,16 +93,22 @@
     ends = jnp.where(me > 0, 1, 0) + jnp.where(me < n - 1, 1, 0)
     pl.semaphore_wait(barrier, ends + copies - 1 + 2)
 
-    def part(c, parts):
-        return pl.ds(c * (width // parts), width // parts)
-
-    def hop(a, side, step, c):
+    def part(c):
+        return pl.ds(c * (width // gather_parts), width // gather_parts)
+
+    def cut(a, c):
+        return pl.ds(sum(cuts[a][:c]), cuts[a][c])
+
+    every = pl.ds(0, width)
+    tr = (tr_back, tr_ahead)
+
+    def hop(a, side, step, columns):
         toward = 1 if side == 0 else -1
         carried = me - toward * (step - 1)
-        columns = part(c, gather_parts)
         block = full.at[a, at_rows(carried), columns]
         return remote(
-            block, block, ss.at[a, side, step - 1, c], rs.at[a, side, step - 1, c],
+            block, block, ss.at[a, side, step - 1],
+            rs.at[a, side, step - 1, columns.start * gather_parts // width],
             "tp", me + toward,
         )
 
@@ -113,7 +125,7 @@
             for side in range(2):
                 @pl.when(sends(side, 1))
                 def _():
-                    hop(a, side, 1, c).start()
+                    hop(a, side, 1, part(c)).start()
 
     def arrive(a, step, parts=None):
         for c in range(gather_parts) if parts is None else parts:
@@ -122,17 +134,17 @@
 
                 @pl.when(gets(side, step))
                 def _():
-                    landed = full.at[a, at_rows(me - toward * step), part(c, gather_parts)]
+                    landed = full.at[a, at_rows(me - toward * step), part(c)]
                     remote(
                         landed, landed,
-                        ss.at[a, side, step - 1, c], rs.at[a, side, step - 1, c], "tp",
+                        ss.at[a, side, step - 1], rs.at[a, side, step - 1, c], "tp",
                         jnp.where(me == 0, 1, me - 1),
                     ).wait_recv()
 
                 if step < n - 1:
                     @pl.when(sends(side, step + 1))
                     def _():
-                        hop(a, side, step + 1, c).start()
+                        hop(a, side, step + 1, part(c)).start()
 
     def square(a, which, index):
         wide = full[a, at_rows(index), :].astype(f32)
@@ -147,7 +159,7 @@
 
     def multiply(a, right, out, which, c=None, kept=0):
         tile = min(256, right.shape[1])
-        features = slice(None) if c is None else part(c, gather_parts)
+        features = slice(None) if c is None else part(c)
 
         @pl.loop(0, right.shape[1] // tile)
         def _(t):
@@ -166,10 +178,10 @@
                 acc[:, held] = product
 
     def allowed(which):
-        numbers = jnp.broadcast_to(docs[which : which + 1, :].astype(f32), (seq, seq))
+        owner = jnp.broadcast_to(docs[which : which + 1, :].astype(f32), (seq, seq))
         i = lax.broadcasted_iota(jnp.int32, (seq, seq), 0)
         j = lax.broadcasted_iota(jnp.int32, (seq, seq), 1)
-        return (j <= i) & (numbers == numbers.T)
+        return (j <= i) & (owner == owner.T)
 
     def stack(ref, g):
         first = g * group
@@ -209,19 +221,20 @@
         dv[:, columns] = dvalues.astype(bf16)
         av[mine, :, columns] = (dvalues * inverse).astype(bf16)
 
-    def copy(a, side, dest, c, first):
-        toward = 1 if side == 0 else -1
-        columns = part(c, sum_parts)
-        target = slots.at[a, side, dest, :, columns]
+    def copy(a, side, dest, c, first, columns):
+        toward = 1 - 2 * side
+        place = dest - 1 + side
+        target = slots.at[a, side, place, :, columns]
         source = sums.at[a, at_rows(dest), columns] if first else target
         return remote(
-            source, target, ts.at[a, side, dest, c], tr.at[a, side, dest, c], "tp", me + toward
+            source, target, ts.at[a, side, place], tr[a].at[side, place, c], "tp", me + toward
         )
 
     def landed(a, side, dest, c):
-        slot = slots.at[a, side, dest, :, part(c, sum_parts)]
+        place = dest - 1 + side
+        slot = slots.at[a, side, place, :, cut(a, c)]
         remote(
-            slot, slot, ts.at[a, side, dest, c], tr.at[a, side, dest, c], "tp",
+            slot, slot, ts.at[a, side, place], tr[a].at[side, place, c], "tp",
             jnp.where(me == 0, 1, me - 1),
         ).wait_recv()
 
@@ -239,38 +252,33 @@
 
             @pl.when(roles(side, dest)[0])
             def _():
-                copy(a, side, dest, c, True).start()
+                copy(a, side, dest, c, True, cut(a, c)).start()
 
     near = jnp.where(2 * me < n, 0, 1)
 
-    def pass_on(a, turn, side):
-        toward = 1 - 2 * side
+    def pass_on(a, turn, side, parts=None):
         dest = jnp.where(side == 0, n - 1 - turn, turn)
+        place = dest - 1 + side
         upward = (side == 0) & (me > 0) & (me < dest)
         downward = (side == 1) & (me < n - 1) & (me > dest)
 
         @pl.when(upward | downward)
         def _():
-            for c in range(sum_parts):
-                columns = part(c, sum_parts)
+            for c in range(len(cuts[a])) if parts is None else parts:
+                columns = cut(a, c)
                 landed(a, side, dest, c)
-                slots[a, side, dest, :, columns] = (
-                    slots[a, side, dest, :, columns].astype(f32)
+                slots[a, side, place, :, columns] = (
+                    slots[a, side, place, :, columns].astype(f32)
                     + sums[a, at_rows(dest), columns].astype(f32)
                 ).astype(bf16)
-                slot = slots.at[a, side, dest, :, columns]
-                remote(
-                    slot, slot, ts.at[a, side, dest, c], tr.at[a, side, dest, c], "tp",
-                    me + toward,
-                ).start()
-
-    def pass_all(a):
-        for side in (near, 1 - near):
-            for turn in range(n - 1):
-                pass_on(a, turn, side)
+                copy(a, side, dest, c, False, columns).start()
+
+    def pass_all(a, side, turns=range(n - 1)):
+        for turn in turns:
+            pass_on(a, turn, side)
 
     def collect(a, c, base):
-        columns = part(c, sum_parts)
+        columns = cut(a, c)
         mine_sum = sums[a, at_rows(me), columns].astype(f32)
         if base is not None:
             mine_sum = mine_sum + full[base, at_rows(me), columns].astype(f32)
@@ -279,14 +287,15 @@
             @pl.when(me > 0 if side == 0 else me < n - 1)
             def _():
                 landed(a, side, me, c)
-                total[:, columns] += slots[a, side, me, :, columns].astype(f32)
-
-    def spread(a, pairs):
-        tile = min(256, width // sum_parts)
-        for c in range(sum_parts):
-            base = c * (width // sum_parts)
-
-            @pl.loop(0, width // sum_parts // tile)
+                total[:, columns] += slots[a, side, me - 1 + side, :, columns].astype(f32)
+
+    def spread(a, pairs, halfway=None):
+        count = len(cuts[a])
+        for c, size in enumerate(cuts[a]):
+            base = sum(cuts[a][:c])
+            tile = math.gcd(256, size)
+
+            @pl.loop(0, size // tile)
             def _(t):
                 features = pl.ds(pl.multiple_of(base + t * tile, tile), tile)
                 acc = None
@@ -296,8 +305,10 @@
                 sums[a, :, features] = acc.astype(bf16)
 
             first_send(a, 0, c)
+            if halfway is not None and c == (count - 1) // 2:
+                halfway()
         for turn in range(1, n - 1):
-            for c in range(sum_parts):
+            for c in range(count):
                 first_send(a, turn, c)
 
     loads[0].wait()
@@ -359,6 +370,7 @@
         for right, out in ((vq, q), (vk, k), (vv, v)):
             multiply(2, right, out, 1, c, kept)
             kept += right.shape[1]
+    pass_all(0, near, range(1))
     for g in range(kv_local):
         heads = jnp.dot(
             probabilities(0, g), head(v, g), preferred_element_type=f32
@@ -366,9 +378,9 @@
         for h in range(group):
             columns = slice((g * group + h) * HEAD, (g * group + h + 1) * HEAD)
             mixed[:, columns] = heads[h * seq : (h + 1) * seq]
-    spread(1, ((mixed, vo),))
-
-    pass_all(0)
+    spread(1, ((mixed, vo),), lambda: pass_all(0, near, range(1, n - 1)))
+    pass_all(0, 1 - near)
+
     for one in trades:
         one.wait()
     tile = min(256, piece)
@@ -382,53 +394,49 @@
                 left, right[...].reshape(copies * seq, right.shape[2])
             )
 
-    handoffs = []
-    for c in range(sum_parts):
+    for c in range(len(cuts[0])):
         collect(0, c, None)
     inverse = inv[0, at_rows(me), :1]
     scaled = full[0, at_rows(me), :].astype(f32) * inverse
     centred = total[...] - scaled * jnp.mean(total[...] * scaled, axis=-1, keepdims=True)
     outgoing[0] = (full[1, at_rows(me), :].astype(f32) + inverse * centred).astype(bf16)
-    for c in range(sum_parts):
-        columns = part(c, sum_parts)
-        handoff = remote(
-            outgoing.at[0, :, columns], grad_out.at[:, columns], hs.at[0, c], hr.at[0, c],
-            "pp", behind,
+
+    def handoff(a, target, device, columns):
+        return remote(
+            outgoing.at[a, :, columns], target.at[:, columns], hs.at[a], hr.at[a], "pp", device
         )
-        handoff.start()
-        handoffs.append(handoff)
-
-    pass_all(1)
-    for c in range(sum_parts):
-        columns = part(c, sum_parts)
+
+    handoff(0, grad_out, behind, every).start()
+
+    pass_on(1, 0, near)
+    for turn in range(1, n):
+        for c in range(len(cuts[1])):
+            pass_on(1, turn - 1, 1 - near, (c,))
+            if turn < n - 1:
+                pass_on(1, turn, near, (c,))
+    for c in range(len(cuts[1])):
+        columns = cut(1, c)
         collect(1, c, 2)
         outgoing[1, :, columns] = total[:, columns].astype(bf16)
-        handoff = remote(
-            outgoing.at[1, :, columns], act_out.at[:, columns], hs.at[1, c], hr.at[1, c],
-            "pp", ahead,
-        )
-        handoff.start()
-        handoffs.append(handoff)
+        handoff(1, act_out, ahead, columns).start()
 
     for a in range(3):
         for step in range(1, n):
-            for c in range(gather_parts):
-                for side in range(2):
-                    @pl.when(sends(side, step))
-                    def _():
-                        hop(a, side, step, c).wait_send()
+            for side in range(2):
+                @pl.when(sends(side, step))
+                def _():
+                    hop(a, side, step, every).wait_send()
     for a in range(2):
         for turn in range(n - 1):
-            for c in range(sum_parts):
-                for side in range(2):
-                    dest = route(side, turn)
-                    first, middle = roles(side, dest)
-
-                    @pl.when(first | middle)
-                    def _():
-                        copy(a, side, dest, c, False).wait_send()
-    for one in handoffs:
-        one.wait()
+            for side in range(2):
+                dest = route(side, turn)
+                first, middle = roles(side, dest)
+
+                @pl.when(first | middle)
+                def _():
+                    copy(a, side, dest, 0, False, every).wait_send()
+    handoff(0, grad_out, behind, every).wait()
+    handoff(1, act_out, ahead, every).wait()
 
 
 def pin(x):
@@ -438,7 +446,7 @@
 def section_call(n, copies, stages, stash, grad, act, docs, wq, wk, wv, wo):
     rows, width = act.shape
     seq = rows * n
-    gather_parts, sum_parts = chunking(rows, width)
+    gather_parts, cuts = chunking(rows, width)
     vmem = pl.BlockSpec(memory_space=pltpu.VMEM)
     hbm = pl.BlockSpec(memory_space=pltpu.HBM)
     heads = wk.shape[1] // HEAD
@@ -450,11 +458,12 @@
     sem = pltpu.SemaphoreType.DMA
     flops = 2 * seq * width * (3 * wq.shape[1] + 3 * wk.shape[1] + 3 * wv.shape[1] + wo.shape[1])
     return pl.pallas_call(
-        functools.partial(section_kernel, n, copies, stages, gather_parts, sum_parts),
+        functools.partial(section_kernel, n, copies, stages, gather_parts, cuts),
         out_shape=outs,
-        in_specs=[hbm] * 3 + [vmem] + [hbm] * 4,
+        in_specs=[hbm] * 8,
         out_specs=[vmem] * len(outs),
         scratch_shapes=[
+            pltpu.VMEM(docs.shape, docs.dtype),
             pltpu.VMEM((3, seq, width), bf16),
             pltpu.VMEM((2, seq, HEAD), f32),
         ]
@@ -467,14 +476,15 @@
         + [
             pltpu.VMEM((seq, held), f32),
             pltpu.VMEM((2, seq, width), bf16),
-            pltpu.VMEM((2, 2, n, rows, width), bf16),
+            pltpu.VMEM((2, 2, n - 1, rows, width), bf16),
             pltpu.VMEM((rows, width), f32),
             pltpu.VMEM((2, rows, width), bf16),
-            sem((7,)),
-            sem((3, 2, n, gather_parts)), sem((3, 2, n, gather_parts)),
-            sem((2, 2, n, sum_parts)), sem((2, 2, n, sum_parts)),
+            sem((8,)),
+            sem((3, 2, n - 1)), sem((3, 2, n - 1, gather_parts)),
+            sem((2, 2, n - 1)),
+            *(sem((2, n - 1, len(sizes))) for sizes in cuts),
             sem((copies, 4)), sem((copies, 4)),
-            sem((2, sum_parts)), sem((2, sum_parts)),
+            sem((2,)), sem((2,)),
         ],
         compiler_params=pltpu.CompilerParams(
             collective_id=0, has_side_effects=True, vmem_limit_bytes=VMEM_LIMIT
@@ -482,7 +492,7 @@
         cost_estimate=pl.CostEstimate(
             flops=flops, bytes_accessed=30_000_000, transcendentals=0
         ),
-    )(*(pin(x) for x in (stash, grad, act)), docs, *(pin(x) for x in (wq, wk, wv, wo)))
+    )(*(pin(x) for x in (stash, grad, act, docs, wq, wk, wv, wo)))
 
 
 def store_kernel(*refs):

time: 92.7 us -> 86 us (0.928)
  Pallas kernels: 91.1 us -> 84.3 us
    pallas_call x1, Pallas kernels: 86.2 us -> 79.4 us  [section_call(): pl.pallas_call(functools.partial(section_kernel, n, copies, stages, gathe...]
where the time goes in v4:
time: 86 us; the launch traced here: 84.9 us
  Pallas kernels  84.3 us (98%)
    pallas_call x1, Pallas kernels, section_call(): pl.pallas_call(functools.partial(section_kernel, n, copies, stages, gathe...  79.4 us
    pallas_call x1, Pallas kernels, store_call(): pl.pallas_call(store_kernel, out_shape=[jax.ShapeDtypeStruct(a.shape, a.d...  4.89 us

profile of v4, /device:TPU:1, one launch (start us, length us, event | category | flops | bytes accessed | tf_op | source)
XLA Modules:
  0.0 84.9 jit_solution(2428287400920555786)
XLA Ops:
  0.6 79.4 %shard_map.119 = (bf16[32,4096]{1,0:T(8,128)(2,1)S(1)}, bf16[32,4096]{1,0:T(8,128)(2,1)S(1)}, f32[2048,1024]{1,0:T(8,128)S(1)}, f32[2048,256]{1,0:T(8,128)S(1)}, f32[2048,256]{1,0:T(8,128)S(1)}) custom-call(bf16[32,4096]{1,0:T(8,128)(2,1)} %bitcast.20, bf16[32,4096]{1,0:T(8,128)(2,1)} %bitcast.21, bf16[32,4096]{1,0:T(8,128)(2,1)} %bitcast.22, ...), custom_call_target="tpu_custom_call" | custom-call | flops 5905580032 | bytes 30000000 | tf_op jit(solution)/shard_map/pallas_call | solution.py:460
  80.0 4.9 %shard_map.120 = (bf16[32,4096]{1,0:T(8,128)(2,1)}, bf16[32,4096]{1,0:T(8,128)(2,1)}, f32[2048,1024]{1,0:T(8,128)}, f32[2048,256]{1,0:T(8,128)}, f32[2048,256]{1,0:T(8,128)}) custom-call(bf16[32,4096]{1,0:T(8,128)(2,1)S(1)} %get-tuple-element.15.refs_0_, bf16[32,4096]{1,0:T(8,128)(2,1)S(1)} %get-tuple-element.16.refs_1_, ...), custom_call_target="tpu_custom_call" | custom-call | flops 10000000 | bytes 26214400 | tf_op jit(solution)/shard_map/pallas_call | solution.py:516

commit v5 on v4

--- a/solution.py
+++ b/solution.py
@@ -37,16 +37,15 @@
 
 def chunking(rows, width):
     if rows * width < 32 * 4096:
-        return 1, ((width,), (width,))
+        return (width,), ((width,), (width,))
     eighth = width // 8
-    return 4, (
-        tuple(eighth * k for k in (1, 1, 2, 2, 2)),
-        tuple(eighth * k for k in (1, 2, 2, 1, 1, 1)),
-    )
+    sizes = ((3, 2, 2, 1), (1, 2, 2, 3), (2, 2, 2, 1, 1))
+    gathered, *summed = (tuple(eighth * k for k in one) for one in sizes)
+    return gathered, tuple(summed)
 
 
 def section_kernel(
-    n, copies, stages, gather_parts, cuts,
+    n, copies, stages, blocks, cuts,
     stash, grad, act, numbers, wq, wk, wv, wo,
     act_out, grad_out, wgq, wgk, wgv,
     docs, full, inv, vq, vk, vv, vo, q, k, v, dm, mixed, probs, dq, dk, dv,
@@ -93,8 +92,10 @@
     ends = jnp.where(me > 0, 1, 0) + jnp.where(me < n - 1, 1, 0)
     pl.semaphore_wait(barrier, ends + copies - 1 + 2)
 
+    gather_parts = len(blocks)
+
     def part(c):
-        return pl.ds(c * (width // gather_parts), width // gather_parts)
+        return pl.ds(sum(blocks[:c]), blocks[c])
 
     def cut(a, c):
         return pl.ds(sum(cuts[a][:c]), cuts[a][c])
@@ -102,13 +103,13 @@
     every = pl.ds(0, width)
     tr = (tr_back, tr_ahead)
 
-    def hop(a, side, step, columns):
+    def hop(a, side, step, c, columns):
         toward = 1 if side == 0 else -1
         carried = me - toward * (step - 1)
         block = full.at[a, at_rows(carried), columns]
         return remote(
             block, block, ss.at[a, side, step - 1],
-            rs.at[a, side, step - 1, columns.start * gather_parts // width],
+            rs.at[a, side, step - 1, c],
             "tp", me + toward,
         )
 
@@ -125,7 +126,7 @@
             for side in range(2):
                 @pl.when(sends(side, 1))
                 def _():
-                    hop(a, side, 1, part(c)).start()
+                    hop(a, side, 1, c, part(c)).start()
 
     def arrive(a, step, parts=None):
         for c in range(gather_parts) if parts is None else parts:
@@ -144,7 +145,7 @@
                 if step < n - 1:
                     @pl.when(sends(side, step + 1))
                     def _():
-                        hop(a, side, step + 1, part(c)).start()
+                        hop(a, side, step + 1, c, part(c)).start()
 
     def square(a, which, index):
         wide = full[a, at_rows(index), :].astype(f32)
@@ -158,7 +159,7 @@
                 square(a, which, me - step if side == 0 else me + step)
 
     def multiply(a, right, out, which, c=None, kept=0):
-        tile = min(256, right.shape[1])
+        tile = math.gcd(1024, right.shape[1])
         features = slice(None) if c is None else part(c)
 
         @pl.loop(0, right.shape[1] // tile)
@@ -291,9 +292,10 @@
 
     def spread(a, pairs, halfway=None):
         count = len(cuts[a])
+        early = 2 if a == 0 and n > 2 and count > 2 else 0
         for c, size in enumerate(cuts[a]):
             base = sum(cuts[a][:c])
-            tile = math.gcd(256, size)
+            tile = math.gcd(512, size)
 
             @pl.loop(0, size // tile)
             def _(t):
@@ -305,11 +307,31 @@
                 sums[a, :, features] = acc.astype(bf16)
 
             first_send(a, 0, c)
+            if c < early:
+                first_send(a, 1, c)
             if halfway is not None and c == (count - 1) // 2:
                 halfway()
         for turn in range(1, n - 1):
-            for c in range(count):
+            for c in range(early if turn == 1 else 0, count):
                 first_send(a, turn, c)
+
+    def gather_sent():
+        for a in range(3):
+            for step in range(1, n):
+                for side in range(2):
+                    @pl.when(sends(side, step))
+                    def _():
+                        hop(a, side, step, 0, every).wait_send()
+
+    def sums_sent(a):
+        for turn in range(n - 1):
+            for side in range(2):
+                dest = route(side, turn)
+                first, middle = roles(side, dest)
+
+                @pl.when(first | middle)
+                def _():
+                    copy(a, side, dest, 0, False, every).wait_send()
 
     loads[0].wait()
     start(0)
@@ -328,7 +350,7 @@
         for offset in range(1, copies):
             other = lax.rem(mine + offset, copies)
             one = remote(
-                source(other), target, dss.at[offset, i], drs.at[offset, i], "dp", other
+                source(other), target, dss.at[offset - 1, i], drs.at[offset - 1, i], "dp", other
             )
             one.start()
             trades.append(one)
@@ -408,34 +430,22 @@
 
     handoff(0, grad_out, behind, every).start()
 
+    gather_sent()
     pass_on(1, 0, near)
     for turn in range(1, n):
         for c in range(len(cuts[1])):
             pass_on(1, turn - 1, 1 - near, (c,))
             if turn < n - 1:
                 pass_on(1, turn, near, (c,))
+    sums_sent(0)
+    handoff(0, grad_out, behind, every).wait()
     for c in range(len(cuts[1])):
         columns = cut(1, c)
         collect(1, c, 2)
         outgoing[1, :, columns] = total[:, columns].astype(bf16)
         handoff(1, act_out, ahead, columns).start()
 
-    for a in range(3):
-        for step in range(1, n):
-            for side in range(2):
-                @pl.when(sends(side, step))
-                def _():
-                    hop(a, side, step, every).wait_send()
-    for a in range(2):
-        for turn in range(n - 1):
-            for side in range(2):
-                dest = route(side, turn)
-                first, middle = roles(side, dest)
-
-                @pl.when(first | middle)
-                def _():
-                    copy(a, side, dest, 0, False, every).wait_send()
-    handoff(0, grad_out, behind, every).wait()
+    sums_sent(1)
     handoff(1, act_out, ahead, every).wait()
 
 
@@ -446,7 +456,7 @@
 def section_call(n, copies, stages, stash, grad, act, docs, wq, wk, wv, wo):
     rows, width = act.shape
     seq = rows * n
-    gather_parts, cuts = chunking(rows, width)
+    blocks, cuts = chunking(rows, width)
     vmem = pl.BlockSpec(memory_space=pltpu.VMEM)
     hbm = pl.BlockSpec(memory_space=pltpu.HBM)
     heads = wk.shape[1] // HEAD
@@ -458,7 +468,7 @@
     sem = pltpu.SemaphoreType.DMA
     flops = 2 * seq * width * (3 * wq.shape[1] + 3 * wk.shape[1] + 3 * wv.shape[1] + wo.shape[1])
     return pl.pallas_call(
-        functools.partial(section_kernel, n, copies, stages, gather_parts, cuts),
+        functools.partial(section_kernel, n, copies, stages, blocks, cuts),
         out_shape=outs,
         in_specs=[hbm] * 8,
         out_specs=[vmem] * len(outs),
@@ -480,10 +490,10 @@
             pltpu.VMEM((rows, width), f32),
             pltpu.VMEM((2, rows, width), bf16),
             sem((8,)),
-            sem((3, 2, n - 1)), sem((3, 2, n - 1, gather_parts)),
+            sem((3, 2, n - 1)), sem((3, 2, n - 1, len(blocks))),
             sem((2, 2, n - 1)),
             *(sem((2, n - 1, len(sizes))) for sizes in cuts),
-            sem((copies, 4)), sem((copies, 4)),
+            sem((copies - 1, 4)), sem((copies - 1, 4)),
             sem((2,)), sem((2,)),
         ],
         compiler_params=pltpu.CompilerParams(
@@ -495,16 +505,22 @@
     )(*(pin(x) for x in (stash, grad, act, docs, wq, wk, wv, wo)))
 
 
+def store_pieces(array):
+    return max(1, array.size * array.dtype.itemsize // 2**21)
+
+
 def store_kernel(*refs):
     count = (len(refs) - 1) // 2
     sems = refs[-1]
     copies = []
-    for i, (source, target) in enumerate(zip(refs[:count], refs[count:-1])):
-        pieces = max(1, source.shape[0] // 512)
+    used = 0
+    for source, target in zip(refs[:count], refs[count:-1]):
+        pieces = store_pieces(source)
         size = source.shape[0] // pieces
         for p in range(pieces):
             where = pl.ds(p * size, size)
-            one = pltpu.make_async_copy(source.at[where], target.at[where], sems.at[i, p])
+            one = pltpu.make_async_copy(source.at[where], target.at[where], sems.at[used])
+            used += 1
             one.start()
             copies.append(one)
     for one in copies:
@@ -512,13 +528,13 @@
 
 
 def store_call(*arrays):
-    pieces = max(1, max(a.shape[0] for a in arrays) // 512)
+    pieces = sum(store_pieces(a) for a in arrays)
     return pl.pallas_call(
         store_kernel,
         out_shape=[jax.ShapeDtypeStruct(a.shape, a.dtype) for a in arrays],
         in_specs=[pl.BlockSpec(memory_space=pltpu.VMEM)] * len(arrays),
         out_specs=[pl.BlockSpec(memory_space=pltpu.HBM)] * len(arrays),
-        scratch_shapes=[pltpu.SemaphoreType.DMA((len(arrays), pieces))],
+        scratch_shapes=[pltpu.SemaphoreType.DMA((pieces,))],
         compiler_params=pltpu.CompilerParams(vmem_limit_bytes=20 * 1024 * 1024),
         cost_estimate=pl.CostEstimate(
             flops=10_000_000, bytes_accessed=sum(2 * a.size * a.dtype.itemsize for a in arrays),

time: 86 us -> 83.4 us (0.970)
  Pallas kernels: 84.3 us -> 81.6 us
    pallas_call x1, Pallas kernels: 79.4 us -> 76.8 us  [section_call(): pl.pallas_call(functools.partial(section_kernel, n, copies, stages, block...]
where the time goes in v5:
time: 83.4 us; the launch traced here: 82.3 us
  Pallas kernels  81.6 us (98%)
    pallas_call x1, Pallas kernels, section_call(): pl.pallas_call(functools.partial(section_kernel, n, copies, stages, block...  76.8 us
    pallas_call x1, Pallas kernels, store_call(): pl.pallas_call(store_kernel, out_shape=[jax.ShapeDtypeStruct(a.shape, a.d...  4.84 us

profile of v5, /device:TPU:1, one launch (start us, length us, event | category | flops | bytes accessed | tf_op | source)
XLA Modules:
  0.0 82.3 jit_solution(18103591252635782329)
XLA Ops:
  0.6 76.8 %shard_map.119 = (bf16[32,4096]{1,0:T(8,128)(2,1)S(1)}, bf16[32,4096]{1,0:T(8,128)(2,1)S(1)}, f32[2048,1024]{1,0:T(8,128)S(1)}, f32[2048,256]{1,0:T(8,128)S(1)}, f32[2048,256]{1,0:T(8,128)S(1)}) custom-call(bf16[32,4096]{1,0:T(8,128)(2,1)} %bitcast.20, bf16[32,4096]{1,0:T(8,128)(2,1)} %bitcast.21, bf16[32,4096]{1,0:T(8,128)(2,1)} %bitcast.22, ...), custom_call_target="tpu_custom_call" | custom-call | flops 5905580032 | bytes 30000000 | tf_op jit(solution)/shard_map/pallas_call | solution.py:470
  77.4 4.8 %shard_map.120 = (bf16[32,4096]{1,0:T(8,128)(2,1)}, bf16[32,4096]{1,0:T(8,128)(2,1)}, f32[2048,1024]{1,0:T(8,128)}, f32[2048,256]{1,0:T(8,128)}, f32[2048,256]{1,0:T(8,128)}) custom-call(bf16[32,4096]{1,0:T(8,128)(2,1)S(1)} %get-tuple-element.15.refs_0_, bf16[32,4096]{1,0:T(8,128)(2,1)S(1)} %get-tuple-element.16.refs_1_, ...), custom_call_target="tpu_custom_call" | custom-call | flops 10000000 | bytes 26214400 | tf_op jit(solution)/shard_map/pallas_call | solution.py:532
